TPU v7x, 32 devices: a whole 2x2x4 slice. The times are simulated.
32 devices in a mesh: dp: 2 (over core), context: 4 (over y, x), expert: 4 (over z).
Axes of the slice: x: 2, y: 2, z: 4, core: 2. Of those that a mesh axis runs over, the one named last changes fastest.
Arguments:
- hidden_in: bfloat16 [2, 2048, 2048], P('dp', ('context', 'expert')), may hold values from -6 to 6
- attn_gain: float32 [2048], replicated, may hold values from 0.5 to 1.5
- w_qkv: bfloat16 [3, 2048, 2048], P(None, None, 'expert'), may hold values from -0.125 to 0.125
- qk_gain: float32 [2, 2048], P(None, 'expert'), may hold values from 0.5 to 1.5
- w_out: bfloat16 [2048, 2048], P('expert'), may hold values from -0.375 to 0.375
- moe_gain: float32 [2048], replicated, may hold values from 0.5 to 1.5
- router: float32 [2048, 16], replicated, may hold values from -0.125 to 0.125
- w_gate: bfloat16 [16, 2048, 1024], P(('context', 'expert')), may hold values from -0.125 to 0.125
- w_up: bfloat16 [16, 2048, 1024], P(('context', 'expert')), may hold values from -0.125 to 0.125
- w_down: bfloat16 [16, 1024, 2048], P(('context', 'expert')), may hold values from -0.75 to 0.75
- expert_ids: int32 [2, 2048, 8], P('dp', ('context', 'expert')), may hold values from 0 to 15, all different within a row; in each aligned block of 128 rows (0 to 127, 128 to 255, ..., all dimensions but the last counted through in order) at most 96 rows name the same one
- grad_out: float32 [2, 2048, 2048], P('dp', ('context', 'expert')), may hold values from -6 to 6
Outputs:
- hidden_out: float32 [2, 2048, 2048], P('dp', ('context', 'expert'))
- grad_in: float32 [2, 2048, 2048], P('dp', ('context', 'expert'))
- attn_gain_grad: float32 [2048], replicated
- w_qkv_grad: float32 [3, 2048, 2048], P(None, None, 'expert')
- qk_gain_grad: float32 [2, 2048], P(None, 'expert')
- w_out_grad: float32 [2048, 2048], P('expert')
- moe_gain_grad: float32 [2048], replicated
- router_grad: float32 [2048, 16], replicated
- w_gate_grad: float32 [16, 2048, 1024], P(('context', 'expert'), 'dp')
- w_up_grad: float32 [16, 2048, 1024], P(('context', 'expert'), 'dp')
- w_down_grad: float32 [16, 1024, 2048], P(('context', 'expert'), 'dp')
Inputs may be any that keep to these rules, and one draw needn't show every extreme that they name: `expert_ids`: each token names 8 different experts. In each aligned block of 128 tokens (the rows of one device) no expert is named more than 96 times, a bound that some block reaches.
All inputs are finite; a program needn't handle non-finite values.
Results may differ from a plain program's by a relative error of at most 0.023.
Values may be sent and summed in bfloat16 or wider, within the bound.
A program may use at most 256 MiB of HBM per device.

v0:
```python
import jax
import jax.numpy as jnp
from jax import lax
from jax.sharding import PartitionSpec as P

HEAD_DIM = 128


norm_eps = 1e-05
rope_base = 10000.0
masked_score = -1e30


def rms_scale(values, gain_vec):
    return (
        values * lax.rsqrt(jnp.mean(values * values, axis=-1, keepdims=True) + norm_eps) * gain_vec
    )


def folded_positions(row_ids, span_rows, block_total):
    block_id = row_ids // span_rows
    offset = row_ids % span_rows
    half_rows = span_rows // 2
    piece_id = jnp.where(offset < half_rows, block_id, 2 * block_total - 1 - block_id)
    return piece_id * half_rows + offset % half_rows


def qk_prep(pair_qk, gain_vec, places):
    row_total = pair_qk.shape[1]
    per_head = pair_qk.reshape(2, row_total, -1, HEAD_DIM)
    scaled = per_head * lax.rsqrt(jnp.mean(per_head * per_head, axis=-1, keepdims=True) + norm_eps)
    scaled = scaled * gain_vec.reshape(2, 1, -1, HEAD_DIM)
    half_dim = HEAD_DIM // 2
    frequency = rope_base ** (-2.0 * jnp.arange(half_dim, dtype=jnp.float32) / HEAD_DIM)
    angles = places.astype(jnp.float32)[:, None] * frequency[None, :]
    cosine = jnp.cos(angles)[None, :, None, :]
    sine_table = jnp.sin(angles)[None, :, None, :]
    first_half = scaled[..., :half_dim]
    second_half = scaled[..., half_dim:]
    turned = jnp.concatenate(
        [
            first_half * cosine - second_half * sine_table,
            second_half * cosine + first_half * sine_table,
        ],
        axis=-1,
    )
    return turned.reshape(2, row_total, -1)


def masked_scores(queries, key_heads, query_places, key_places, score_scale):
    scores = (
        jnp.einsum("qhd,khd->hqk", queries, key_heads, preferred_element_type=jnp.float32)
        * score_scale
    )
    return jnp.where(key_places[None, None, :] <= query_places[None, :, None], scores, masked_score)


def contract(left, right, left_dim, right_dim):
    return lax.dot_general(
        left, right, (((left_dim,), (right_dim,)), ((), ())), preferred_element_type=jnp.float32
    )


def on_device(
    hidden_in,
    attn_gain,
    w_qkv,
    qk_gain,
    w_out,
    moe_gain,
    router,
    w_gate,
    w_up,
    w_down,
    expert_ids,
    grad_out,
):
    tokens = hidden_in[0].astype(jnp.float32)
    tok_count = tokens.shape[0]
    model_width = tokens.shape[1]
    context_size = lax.axis_size("context")
    expert_size = lax.axis_size("expert")
    span_rows = tok_count * expert_size
    seq_rows = span_rows * context_size
    context_index = lax.axis_index("context")
    local_places = folded_positions(
        context_index * span_rows + jnp.arange(span_rows, dtype=jnp.int32), span_rows, context_size
    )
    key_places = folded_positions(jnp.arange(seq_rows, dtype=jnp.int32), span_rows, context_size)
    score_scale = HEAD_DIM ** (-0.5)
    normed_b = rms_scale(tokens, attn_gain).astype(jnp.bfloat16)
    gathered_in = lax.all_gather(normed_b, "expert", axis=0, tiled=True)
    projected = jnp.einsum(
        "rd,kdf->krf", gathered_in, w_qkv[:2], preferred_element_type=jnp.float32
    )
    value_local = jnp.dot(gathered_in, w_qkv[2], preferred_element_type=jnp.float32).astype(
        jnp.bfloat16
    )
    feat_width = projected.shape[2]
    heads_here = feat_width // HEAD_DIM

    def prep_local(pair_qk, gain_vec):
        return qk_prep(pair_qk, gain_vec, local_places)

    rotated = prep_local(projected, qk_gain).astype(jnp.bfloat16)
    keys_all, values_all = (
        lax.all_gather(rotated[1], "context", axis=0, tiled=True),
        lax.all_gather(value_local, "context", axis=0, tiled=True),
    )
    key_heads = keys_all.reshape(seq_rows, heads_here, HEAD_DIM)
    value_heads = values_all.reshape(seq_rows, heads_here, HEAD_DIM)
    block_rows = min(512, span_rows)
    block_count = span_rows // block_rows
    key_count = seq_rows // block_rows
    key_lowest = jnp.min(key_places.reshape(key_count, block_rows), axis=1)
    query_blocks = rotated[0].reshape(block_count, block_rows, heads_here, HEAD_DIM)
    place_blocks = local_places.reshape(block_count, block_rows)

    def key_piece(kb):
        start = kb * block_rows
        return (
            lax.dynamic_slice_in_dim(key_heads, start, block_rows, 0),
            lax.dynamic_slice_in_dim(value_heads, start, block_rows, 0),
            lax.dynamic_slice_in_dim(key_places, start, block_rows, 0),
        )

    def attend_blocks(members):
        queries, query_places = members
        query_top = jnp.max(query_places)

        def stat_step(kb, carry):

            def stat_live(state):
                run_max, run_sum = state
                key_blk, value_blk, kplace = key_piece(kb)
                scores = masked_scores(queries, key_blk, query_places, kplace, score_scale)
                new_max = jnp.maximum(run_max, jnp.max(scores, axis=-1))
                new_sum = run_sum * jnp.exp(run_max - new_max) + jnp.sum(
                    jnp.exp(scores - new_max[..., None]), axis=-1
                )
                return (new_max, new_sum)

            return lax.cond(key_lowest[kb] <= query_top, stat_live, lambda state: state, carry)

        start_stat = (
            jnp.full((heads_here, block_rows), masked_score, jnp.float32),
            jnp.zeros((heads_here, block_rows), jnp.float32),
        )
        run_max, run_sum = lax.fori_loop(0, key_count, stat_step, start_stat)
        log_total = run_max + jnp.log(run_sum)

        def value_step(kb, acc):

            def value_live(total):
                key_blk, value_blk, kplace = key_piece(kb)
                scores = masked_scores(queries, key_blk, query_places, kplace, score_scale)
                prob_b = jnp.exp(scores - log_total[..., None]).astype(jnp.bfloat16)
                return total + jnp.einsum(
                    "hqk,khd->qhd", prob_b, value_blk, preferred_element_type=jnp.float32
                )

            return lax.cond(key_lowest[kb] <= query_top, value_live, lambda total: total, acc)

        result = lax.fori_loop(
            0, key_count, value_step, jnp.zeros((block_rows, heads_here, HEAD_DIM), jnp.float32)
        )
        return (result.astype(jnp.bfloat16), log_total)

    attended, log_totals = lax.map(attend_blocks, (query_blocks, place_blocks))
    attended = attended.reshape(span_rows, feat_width)
    piece_rows = attended
    branch_out = lax.psum_scatter(
        jnp.dot(piece_rows, w_out, preferred_element_type=jnp.float32).astype(jnp.bfloat16),
        "expert",
        scatter_dimension=0,
        tiled=True,
    ).astype(jnp.float32)
    resid = tokens + branch_out
    mixed_in = rms_scale(resid, moe_gain)
    logits = jnp.dot(
        mixed_in, router, precision=lax.Precision.HIGHEST, preferred_element_type=jnp.float32
    )
    gate_probs = jax.nn.softmax(logits, axis=-1)
    chosen = expert_ids[0]
    top_count = chosen.shape[1]
    expert_count = router.shape[1]
    picked = chosen[:, :, None] == jnp.arange(expert_count, dtype=jnp.int32)[None, None, :]
    weights = jnp.sum(jnp.where(picked, gate_probs[:, None, :], 0.0), axis=-1)
    assign_count = tok_count * top_count
    flat_pick = picked.reshape(assign_count, expert_count).astype(jnp.int32)
    slot_index = jnp.sum((jnp.cumsum(flat_pick, axis=0) - flat_pick) * flat_pick, axis=-1)
    capacity = 3 * tok_count * top_count // (2 * expert_count)
    target = chosen.reshape(-1) * capacity + slot_index
    expert_in = mixed_in.astype(jnp.bfloat16)
    empty_rows = jnp.zeros((expert_count * capacity, model_width), jnp.bfloat16)
    sending = (
        empty_rows.at[target]
        .set(jnp.repeat(expert_in, top_count, axis=0))
        .reshape(expert_count, capacity, model_width)
    )
    arrived = lax.all_to_all(
        sending, ("context", "expert"), split_axis=0, concat_axis=0, tiled=True
    )
    in_shape = arrived.shape
    row_block = arrived.reshape(-1, model_width)
    gate_pre = jnp.dot(row_block, w_gate[0], preferred_element_type=jnp.float32)
    up_pre = jnp.dot(row_block, w_up[0], preferred_element_type=jnp.float32)
    hidden = (jax.nn.silu(gate_pre) * up_pre).astype(jnp.bfloat16)
    result = (
        jnp.dot(hidden, w_down[0], preferred_element_type=jnp.float32)
        .astype(jnp.bfloat16)
        .reshape(in_shape)
    )
    dispatched = lax.all_to_all(
        result, ("context", "expert"), split_axis=0, concat_axis=0, tiled=True
    )
    expert_out = dispatched.reshape(expert_count * capacity, model_width)[target].reshape(
        tok_count, top_count, model_width
    )
    hidden_out = resid + jnp.sum(weights[:, :, None] * expert_out, axis=1)
    upstream = grad_out[0]
    d_weights = jnp.sum(expert_out * upstream[:, None, :], axis=-1)
    grad_outb = (weights[:, :, None] * upstream[:, None, :]).astype(jnp.bfloat16)
    grad_sending = (
        empty_rows.at[target]
        .set(grad_outb.reshape(assign_count, model_width))
        .reshape(expert_count, capacity, model_width)
    )
    grad_arrived, arrived_all = (
        lax.all_to_all(
            grad_sending, ("context", "expert"), split_axis=0, concat_axis=0, tiled=True
        ),
        lax.all_to_all(sending, ("context", "expert"), split_axis=0, concat_axis=0, tiled=True),
    )
    row_block = arrived_all.reshape(-1, model_width)
    grad_block = grad_arrived.reshape(-1, model_width)
    gate_pre = jnp.dot(row_block, w_gate[0], preferred_element_type=jnp.float32)
    up_pre = jnp.dot(row_block, w_up[0], preferred_element_type=jnp.float32)
    sigmoid_g = jax.nn.sigmoid(gate_pre)
    activated = gate_pre * sigmoid_g
    hidden = (activated * up_pre).astype(jnp.bfloat16)
    grad_hidden = contract(grad_block, w_down[0], 1, 1)
    down_grad = contract(hidden, grad_block, 0, 0)
    grad_gate = (grad_hidden * up_pre * sigmoid_g * (1.0 + gate_pre * (1.0 - sigmoid_g))).astype(
        jnp.bfloat16
    )
    grad_up = (grad_hidden * activated).astype(jnp.bfloat16)
    gate_grad = contract(row_block, grad_gate, 0, 0)
    up_grad = contract(row_block, grad_up, 0, 0)
    grad_rows = (contract(grad_gate, w_gate[0], 1, 1) + contract(grad_up, w_up[0], 1, 1)).astype(
        jnp.bfloat16
    )
    grad_back = lax.all_to_all(
        grad_rows.reshape(grad_arrived.shape),
        ("context", "expert"),
        split_axis=0,
        concat_axis=0,
        tiled=True,
    )
    grad_expert_in = grad_back.reshape(expert_count * capacity, model_width)[target].reshape(
        tok_count, top_count, model_width
    )
    mixed_grad_experts = jnp.sum(grad_expert_in.astype(jnp.float32), axis=1)
    gate_sum, up_sum, down_sum = (
        lax.psum_scatter(
            gate_grad[None].astype(jnp.bfloat16), "dp", scatter_dimension=1, tiled=True
        ).astype(jnp.float32),
        lax.psum_scatter(
            up_grad[None].astype(jnp.bfloat16), "dp", scatter_dimension=1, tiled=True
        ).astype(jnp.float32),
        lax.psum_scatter(
            down_grad[None].astype(jnp.bfloat16), "dp", scatter_dimension=1, tiled=True
        ).astype(jnp.float32),
    )
    d_gates = jnp.sum(jnp.where(picked, d_weights[:, :, None], 0.0), axis=1)
    d_logits = gate_probs * (d_gates - jnp.sum(gate_probs * d_gates, axis=-1, keepdims=True))
    router_part = lax.dot_general(
        mixed_in,
        d_logits,
        (((0,), (0,)), ((), ())),
        precision=lax.Precision.HIGHEST,
        preferred_element_type=jnp.float32,
    )
    d_mixed = mixed_grad_experts + lax.dot_general(
        d_logits,
        router,
        (((1,), (1,)), ((), ())),
        precision=lax.Precision.HIGHEST,
        preferred_element_type=jnp.float32,
    )
    _, second_pull = jax.vjp(rms_scale, resid, moe_gain)
    resid_part, moe_gain_part = second_pull(d_mixed)
    d_resid = upstream + resid_part
    resid_b = d_resid.astype(jnp.bfloat16)
    grad_gathered = lax.all_gather(resid_b, "expert", axis=0, tiled=True)
    out_grad = contract(attended, grad_gathered, 0, 0)
    d_attended = contract(grad_gathered, w_out, 1, 1).astype(jnp.bfloat16)
    grad_blocks = d_attended.reshape(block_count, block_rows, heads_here, HEAD_DIM)

    def backward_block(totals, members):
        query_blk, grad_blk, place_blk, total_blk = members
        query_top = jnp.max(place_blk)

        def dot_step(kb, acc):

            def dot_live(total):
                key_blk, value_blk, kplace = key_piece(kb)
                scores = masked_scores(query_blk, key_blk, place_blk, kplace, score_scale)
                prob_exact = jnp.exp(scores - total_blk[:, :, None])
                d_probs = jnp.einsum(
                    "qhd,khd->hqk", grad_blk, value_blk, preferred_element_type=jnp.float32
                )
                return total + jnp.sum(prob_exact * d_probs, axis=-1)

            return lax.cond(key_lowest[kb] <= query_top, dot_live, lambda total: total, acc)

        row_dot = lax.fori_loop(
            0, key_count, dot_step, jnp.zeros((heads_here, block_rows), jnp.float32)
        )

        def grad_step(kb, carry):

            def grad_live(state):
                key_acc, value_acc, query_acc = state
                start = kb * block_rows
                key_blk, value_blk, kplace = key_piece(kb)
                scores = masked_scores(query_blk, key_blk, place_blk, kplace, score_scale)
                prob_exact = jnp.exp(scores - total_blk[:, :, None])
                prob_b = prob_exact.astype(jnp.bfloat16)
                d_probs = jnp.einsum(
                    "qhd,khd->hqk", grad_blk, value_blk, preferred_element_type=jnp.float32
                )
                d_scores = (prob_exact * (d_probs - row_dot[..., None]) * score_scale).astype(
                    jnp.bfloat16
                )
                query_acc = query_acc + jnp.einsum(
                    "hqk,khd->qhd", d_scores, key_blk, preferred_element_type=jnp.float32
                )
                key_add = jnp.einsum(
                    "hqk,qhd->khd", d_scores, query_blk, preferred_element_type=jnp.float32
                )
                value_add = jnp.einsum(
                    "hqk,qhd->khd", prob_b, grad_blk, preferred_element_type=jnp.float32
                )
                key_acc = lax.dynamic_update_slice_in_dim(
                    key_acc,
                    lax.dynamic_slice_in_dim(key_acc, start, block_rows, 0) + key_add,
                    start,
                    0,
                )
                value_acc = lax.dynamic_update_slice_in_dim(
                    value_acc,
                    lax.dynamic_slice_in_dim(value_acc, start, block_rows, 0) + value_add,
                    start,
                    0,
                )
                return (key_acc, value_acc, query_acc)

            return lax.cond(key_lowest[kb] <= query_top, grad_live, lambda state: state, carry)

        start_grad = (
            totals[0],
            totals[1],
            jnp.zeros((block_rows, heads_here, HEAD_DIM), jnp.float32),
        )
        key_acc, value_acc, d_query = lax.fori_loop(0, key_count, grad_step, start_grad)
        return ((key_acc, value_acc), d_query)

    zero_heads = jnp.zeros((seq_rows, heads_here, HEAD_DIM), jnp.float32)
    (key_acc, value_acc), d_queries = lax.scan(
        backward_block,
        (zero_heads, zero_heads),
        (query_blocks, grad_blocks, place_blocks, log_totals),
    )
    key_grad, value_grad = (
        lax.psum_scatter(
            key_acc.reshape(seq_rows, feat_width).astype(jnp.bfloat16),
            "context",
            scatter_dimension=0,
            tiled=True,
        ).astype(jnp.float32),
        lax.psum_scatter(
            value_acc.reshape(seq_rows, feat_width).astype(jnp.bfloat16),
            "context",
            scatter_dimension=0,
            tiled=True,
        ).astype(jnp.float32),
    )
    d_rotated = jnp.stack([d_queries.reshape(span_rows, feat_width), key_grad])
    _, prep_pull = jax.vjp(prep_local, projected, qk_gain)
    d_pair, qk_part = prep_pull(d_rotated)
    d_proj = jnp.concatenate([d_pair, value_grad[None]], axis=0).astype(jnp.bfloat16)
    qkv_grad = jnp.einsum("rd,krf->kdf", gathered_in, d_proj, preferred_element_type=jnp.float32)
    piece_rows = d_proj
    d_normed = lax.psum_scatter(
        jnp.einsum("krf,kdf->rd", piece_rows, w_qkv, preferred_element_type=jnp.float32).astype(
            jnp.bfloat16
        ),
        "expert",
        scatter_dimension=0,
        tiled=True,
    ).astype(jnp.float32)
    _, first_pull = jax.vjp(rms_scale, tokens, attn_gain)
    token_part, attn_gain_part = first_pull(d_normed)
    grad_in = d_resid + token_part
    qkv_sum, out_sum, qk_sum = (
        lax.psum(qkv_grad.astype(jnp.bfloat16), ("dp", "context")).astype(jnp.float32),
        lax.psum(out_grad.astype(jnp.bfloat16), ("dp", "context")).astype(jnp.float32),
        lax.psum(qk_part.astype(jnp.bfloat16), ("dp", "context")).astype(jnp.float32),
    )
    attn_sum, moe_sum, router_sum = lax.psum(
        (attn_gain_part, moe_gain_part, router_part), ("dp", "context", "expert")
    )
    return (
        hidden_out[None],
        grad_in[None],
        attn_sum,
        qkv_sum,
        qk_sum,
        out_sum,
        moe_sum,
        router_sum,
        gate_sum,
        up_sum,
        down_sum,
    )


def solution(mesh):
    placed = (
        P("dp", ("context", "expert"), None),
        P(),
        P(None, None, "expert"),
        P(None, "expert"),
        P("expert", None),
        P(),
        P(),
        P(("context", "expert"), None, None),
        P(("context", "expert"), None, None),
        P(("context", "expert"), None, None),
        P("dp", ("context", "expert"), None),
        P("dp", ("context", "expert"), None),
    )
    return jax.shard_map(
        on_device,
        mesh=mesh,
        in_specs=placed,
        out_specs=(
            P("dp", ("context", "expert"), None),
            P("dp", ("context", "expert"), None),
            P(),
            P(None, None, "expert"),
            P(None, "expert"),
            P("expert", None),
            P(),
            P(),
            P(("context", "expert"), "dp", None),
            P(("context", "expert"), "dp", None),
            P(("context", "expert"), "dp", None),
        ),
        check_vma=False,
    )
```

profile of v0, /device:TPU:0, one launch (start us, length us, event | category | flops | bytes accessed | tf_op | source)
XLA Modules:
  0.0 1491.0 jit_solution(3097581100040140661)
XLA Ops:
  12.0 47.2 %all-gather.5.cloned.1.call-done = bf16[512,2048]{1,0:T(8,128)(2,1)} async-done(((bf16[128,2048]{1,0:T(8,128)(2,1)}), bf16[512,2048]{1,0:T(8,128)(2,1)}) %all-gather.5.cloned.1.call-update) | async-done | bytes 2097168 | tf_op jit(solution)/shard_map/all_gather | solution.py:92
  59.2 5.2 multiply_reduce_fusion.2
  66.5 4.3 fusion.172
  72.2 28.3 %all-gather.9.cloned.1.call-done = bf16[2048,512]{0,1:T(8,128)(2,1)} async-done(((bf16[512,512]{0,1:T(8,128)(2,1)}), bf16[2048,512]{0,1:T(8,128)(2,1)}) %all-gather.9.cloned.1.call-update) | async-done | bytes 2097168 | tf_op jit(solution)/shard_map/all_gather | solution.py:107
  104.4 21.0 %while.94 = (s32[]{:T(128)}, f32[4,512]{1,0:T(4,128)S(1)}, f32[4,512]{1,0:T(4,128)S(1)}, s32[4]{0:T(128)S(1)}, s32[]{:T(128)}, /*index=5*/bf16[2048,4,128]{2,0,1...) while((s32[]{:T(128)}, f32[4,512]{1,0:T(4,128)S(1)}, ...), condition=%wide.region_9.10_spmd.clone, body=%wide.region_4.9_spmd.clone.sunk | while | flops 276112384 | bytes 10422733 | solution.py:149
  125.4 12.7 all-gather.7.cloned.1.call-done
  143.1 25.9 %while.95 = (s32[]{:T(128)}, f32[512,4,128]{0,2,1:T(8,128)}, s32[4]{0:T(128)S(1)}, s32[]{:T(128)}, bf16[2048,4,128]{0,2,1:T(8,128)(2,1)}, /*index=5*/bf16[2048,4...) while((s32[]{:T(128)}, f32[512,4,128]{0,2,1:T(8,128)}, ...), condition=%wide.region_13.14_spmd.clone, body=%wide.region_10.13_spmd.clone.sunk | while | flops 541660160 | bytes 4296121 | solution.py:164
  145.1 4.5 conditional.13
  151.6 4.5 conditional.13
  151.9 4.1 fusion.42
  158.1 4.5 conditional.13
  164.5 4.5 conditional.13
  164.9 4.1 fusion.42
  174.3 4.5 reduce-window.6
  179.3 38.3 %reduce-scatter.8.cloned.1.call-done = bf16[128,2048]{1,0:T(8,128)(2,1)} async-done(((bf16[512,2048]{1,0:T(8,128)(2,1)}), bf16[128,2048]{1,0:T(8,128)(2,1)}) %reduce-scatter.8.cloned.1.call-update) | async-done | bytes 524304 | tf_op jit(solution)/shard_map/reduce_scatter | solution.py:172
  220.9 11.1 scatter_custom_fusion
  232.0 5.0 all-to-all-start
  239.5 11.0 scatter_custom_fusion.1
  250.4 135.8 %all-to-all-done = bf16[16,96,2048]{2,1,0:T(8,128)(2,1)} async-done(((bf16[16,96,2048]{2,1,0:T(8,128)(2,1)}), bf16[16,96,2048]{2,1,0:T(8,128)(2,1)}, u32[]{:S(2)}, u32[]{:S(2)}) %all-to-all-start) | async-done | bytes 6291488 | tf_op jit(solution)/shard_map/all_to_all | solution.py:201
  386.2 4.8 all-to-all-start.2
  391.1 11.8 fusion.151
  402.9 10.4 fusion.155
  413.2 129.1 %all-to-all-done.2 = bf16[16,96,2048]{2,1,0:T(8,128)(2,1)} async-done(((bf16[16,96,2048]{2,1,0:T(8,128)(2,1)}), bf16[16,96,2048]{2,1,0:T(8,128)(2,1)}, u32[]{:S(2)}, u32[]{:S(2)}) %all-to-all-start.2) | async-done | bytes 6291488 | tf_op jit(solution)/shard_map/all_to_all | solution.py:230
  542.4 17.7 %multiply_convert_fusion = (bf16[1536,1024]{1,0:T(8,128)(2,1)}, bf16[1536,1024]{1,0:T(8,128)(2,1)}, bf16[1536,1024]{1,0:T(8,128)(2,1)S(1)}) fusion(f32[1536,1024]{1,0:T(8,128)} %fusion.155, f32[1536,1024]{1,0:T(8,128)} %fusion.151, bf16[1536,2048]{1,0:T(8,128)(2,1)} %bitcast.39, bf16[1,1024,2048]{2,1,0:T(8,128)(2,1)} %param.37), kind=kOutput, calls=%fused_computation.248 | convolution fusion | flops 6466043904 | bytes 32505856 | tf_op jit(solution)/shard_map/dot_general | solution.py:59
  560.0 8.8 convolution_convert_fusion
  568.8 5.1 all-to-all-start.1
  573.9 12.4 fusion.153
  586.4 11.5 add_convert_fusion
  597.8 127.8 %all-to-all-done.1 = bf16[16,96,2048]{2,1,0:T(8,128)(2,1)} async-done(((bf16[16,96,2048]{2,1,0:T(8,128)(2,1)}), bf16[16,96,2048]{2,1,0:T(8,128)(2,1)}, u32[]{:S(2)}, u32[]{:S(2)}) %all-to-all-start.1) | async-done | bytes 6291488 | tf_op jit(solution)/shard_map/all_to_all | solution.py:214
  725.6 4.6 all-to-all-start.3
  730.3 12.4 gather_fusion
  742.8 5.9 fusion.142
  748.8 133.2 %all-to-all-done.3 = bf16[16,96,2048]{2,1,0:T(8,128)(2,1)} async-done(((bf16[16,96,2048]{2,1,0:T(8,128)(2,1)}), bf16[16,96,2048]{2,1,0:T(8,128)(2,1)}, u32[]{:S(2)}, u32[]{:S(2)}) %all-to-all-start.3) | async-done | bytes 6291488 | tf_op jit(solution)/shard_map/all_to_all | solution.py:253
  882.0 12.4 gather_fusion.1
  894.4 5.2 convert_reduce_fusion
  907.3 38.2 %all-gather.11.cloned.1.call-done = bf16[512,2048]{1,0:T(8,128)(2,1)} async-done(((bf16[128,2048]{1,0:T(8,128)(2,1)}), bf16[512,2048]{1,0:T(8,128)(2,1)}) %all-gather.11.cloned.1.call-update) | async-done | bytes 2097168 | tf_op jit(solution)/shard_map/all_gather | solution.py:295
  951.2 27.1 %while.96 = (s32[]{:T(128)}, f32[4,512]{1,0:T(4,128)S(1)}, s32[4]{0:T(128)S(1)}, s32[]{:T(128)}, bf16[2048,4,128]{2,0,1:T(8,128)(2,1)}, /*index=5*/bf16[512,4,12...) while((s32[]{:T(128)}, f32[4,512]{1,0:T(4,128)S(1)}, ...), condition=%wide.region_34.35_spmd.clone, body=%wide.region_30.34_spmd.clone.sunk | while | flops 542446592 | bytes 11143633 | solution.py:317
  953.2 4.7 conditional.14
  959.9 4.7 conditional.14
  966.7 4.7 conditional.14
  973.5 4.7 conditional.14
  983.9 65.6 %while.97 = (s32[]{:T(128)}, f32[2048,4,128]{2,0,1:T(8,128)}, f32[2048,4,128]{2,0,1:T(8,128)}, f32[512,4,128]{0,2,1:T(8,128)}, s32[4]{0:T(128)S(1)}, /*index=5*/...) while((s32[]{:T(128)}, f32[2048,4,128]{2,0,1:T(8,128)}, ...), condition=%wide.region_38.39_spmd.clone, body=%wide.region_35.38_spmd.clone.sunk | while | flops 1354830848 | bytes 29739580 | solution.py:366
  986.0 14.3 conditional.15
  1002.4 14.3 conditional.15
  1018.8 14.3 conditional.15
  1035.2 14.3 conditional.15
  1049.5 4.6 copy.130
  1058.2 11.5 convert_bitcast_fusion.1
  1069.8 11.2 convert_bitcast_fusion.2
  1081.1 11.2 convert_bitcast_fusion.3
  1099.5 27.5 %reduce-scatter.12.cloned.1.call-done = bf16[512,512]{1,0:T(8,128)(2,1)} async-done(((bf16[2048,512]{1,0:T(8,128)(2,1)}), bf16[512,512]{1,0:T(8,128)(2,1)}) %reduce-scatter.12.cloned.1.call-update) | async-done | bytes 524304 | tf_op jit(solution)/shard_map/reduce_scatter | solution.py:382
  1127.0 7.8 bitcast_convert_fusion
  1134.9 4.9 convolution_convert_fusion.1
  1139.8 5.4 convert_bitcast_fusion
  1145.3 4.1 convert_element_type.239
  1149.4 8.8 reduce-scatter.18.cloned.1.call-done
  1162.3 12.0 reduce-scatter.16.cloned.1.call-done
  1179.9 14.7 psum.44
  1195.2 26.9 %reduce-scatter.14.cloned.1.call-done = bf16[128,2048]{1,0:T(8,128)(2,1)} async-done(((bf16[512,2048]{1,0:T(8,128)(2,1)}), bf16[128,2048]{1,0:T(8,128)(2,1)}) %reduce-scatter.14.cloned.1.call-update) | async-done | bytes 524304 | tf_op jit(solution)/shard_map/reduce_scatter | solution.py:395
  1227.1 124.6 %all-reduce.9.cloned.1.call-done = (bf16[3,2048,512]{1,2,0:T(8,128)(2,1)}, bf16[512,2048]{1,0:T(8,128)(2,1)}) async-done(((bf16[3,2048,512]{1,2,0:T(8,128)(2,1)}, bf16[512,2048]{1,0:T(8,128)(2,1)}), (bf16[3,2048,512]{1,2,0:T(8,128)(2,1)}, bf16[512,2048]{1,0:T(8,128)(2,1)})) %all-reduce.9.cloned.1.call-update) | async-done | bytes 8388624 | tf_op jit(solution)/shard_map/psum | solution.py:407
  1351.7 4.1 convert_element_type.230
  1355.8 9.6 copy.134
  1365.4 39.6 %all-reduce.2 = (f32[2048]{0:T(1024)}, f32[2048]{0:T(1024)}) all-reduce(f32[2048]{0:T(1024)S(1)} %get-tuple-element.1748, f32[2048]{0:T(1024)S(1)} %copy-done.27), channel_id=1, replica_groups=mesh['dp'=2,'context'=4,'expert'=4] {'dp','context','expert'}, use_global_device_ids=true, to_apply=%region_45.46 | all-reduce | flops 4096 | bytes 32768 | tf_op jit(solution)/shard_map/psum | solution.py:411
  1405.0 77.4 %all-reduce.7.cloned.1.call-done = f32[2048,16]{0,1:T(8,128)} async-done(((f32[2048,16]{0,1:T(8,128)}), f32[2048,16]{0,1:T(8,128)}) %all-reduce.7.cloned.1.call-update) | async-done | bytes 131088 | tf_op jit(solution)/shard_map/psum | solution.py:411
  (416 shorter events, 197.1 us)
Async XLA Ops:
  7.2 164.0 %copy-start = (bf16[512,2048]{1,0:T(8,128)(2,1)S(1)}, bf16[512,2048]{1,0:T(8,128)(2,1)}, u32[]{:S(2)}) copy-start(bf16[512,2048]{1,0:T(8,128)(2,1)} %param.32) | copy-start | bytes 6291460
  7.2 52.0 %all-gather.5.cloned.1.call-start = ((), (), s32[]{:S(2)}) async-start(), calls=%async_computation.11 | async-start | bytes 2621440 | tf_op jit(solution)/shard_map/all_gather | solution.py:92
  8.6 55.8 %copy-start.30 = (f32[128]{0:T(128)}, f32[128]{0:T(128)S(1)}, u32[]{:S(2)}) copy-start(f32[128]{0:T(128)S(1)} %fusion.182) | copy-start | bytes 1540
  8.6 2.8 copy-start.28
  10.7 89.8 %all-gather.9.cloned.1.call-start = ((), (), s32[]{:S(2)}) async-start(), calls=%async_computation.13 | async-start | bytes 2621440 | tf_op jit(solution)/shard_map/all_gather | solution.py:107
  11.4 53.1 %copy-start.25 = (f32[2,4,128]{2,1,0:T(4,128)}, f32[2,4,128]{2,1,0:T(4,128)S(1)}, u32[]{:S(2)}) copy-start(f32[2,4,128]{2,1,0:T(4,128)S(1)} %mul.429) | copy-start | bytes 12292
  12.0 53.2 %copy-start.11 = (f32[512,64]{0,1:T(8,128)}, f32[512,64]{0,1:T(8,128)S(1)}, u32[]{:S(2)}) copy-start(f32[512,64]{0,1:T(8,128)S(1)} %get-tuple-element.1871) | copy-start | bytes 393220
  12.0 53.2 %copy-start.13 = (f32[512,64]{0,1:T(8,128)}, f32[512,64]{0,1:T(8,128)S(1)}, u32[]{:S(2)}) copy-start(f32[512,64]{0,1:T(8,128)S(1)} %get-tuple-element.1872) | copy-start | bytes 393220
  64.5 0.6 copy-start.22
  64.5 2.0 copy-start.2
  64.5 0.7 copy-start.17
  66.5 71.6 %all-gather.7.cloned.1.call-start = ((), (), s32[]{:S(2)}) async-start(), calls=%async_computation.12 | async-start | bytes 2621440 | tf_op jit(solution)/shard_map/all_gather | solution.py:108
  70.8 146.8 %reduce-scatter.8.cloned.1.call-start = ((), (), s32[]{:S(2)}) async-start(), calls=%async_computation.14 | async-start | bytes 2621440 | tf_op jit(solution)/shard_map/reduce_scatter | solution.py:172
  170.3 0.8 copy-start.15
  170.3 3.4 copy-start.24
  171.1 46.5 %copy-start.4 = (bf16[1,128,2048]{2,1,0:T(8,128)(2,1)S(1)}, bf16[1,128,2048]{2,1,0:T(8,128)(2,1)}, u32[]{:S(2)}) copy-start(bf16[1,128,2048]{2,1,0:T(8,128)(2,1)} %param.28) | copy-start | bytes 1572868
  171.1 47.8 %copy-start.20 = (f32[2048]{0:T(1024)S(1)}, f32[2048]{0:T(1024)}, u32[]{:S(2)}) copy-start(f32[2048]{0:T(1024)} %param.33) | copy-start | bytes 24580
  232.0 5.0 copy-start.19
  232.0 154.2 %all-to-all-start = ((bf16[16,96,2048]{2,1,0:T(8,128)(2,1)}), bf16[16,96,2048]{2,1,0:T(8,128)(2,1)}, u32[]{:S(2)}, u32[]{:S(2)}) async-start(bf16[16,96,2048]{2,1,0:T(8,128)(2,1)} %bitcast.288), calls=%async_computation.1 | async-start | bytes 12582912 | tf_op jit(solution)/shard_map/all_to_all | solution.py:201
  386.2 156.1 %all-to-all-start.2 = ((bf16[16,96,2048]{2,1,0:T(8,128)(2,1)}), bf16[16,96,2048]{2,1,0:T(8,128)(2,1)}, u32[]{:S(2)}, u32[]{:S(2)}) async-start(bf16[16,96,2048]{2,1,0:T(8,128)(2,1)} %bitcast.289), calls=%async_computation.3 | async-start | bytes 12582912 | tf_op jit(solution)/shard_map/all_to_all | solution.py:230
  391.1 11.8 copy-start.33
  542.4 17.7 %copy-start.32 = (bf16[1,1024,2048]{2,1,0:T(8,128)(2,1)S(1)}, bf16[1,1024,2048]{2,1,0:T(8,128)(2,1)}, u32[]{:S(2)}) copy-start(bf16[1,1024,2048]{2,1,0:T(8,128)(2,1)} %param.37) | copy-start | bytes 12582916
  560.0 8.8 copy-start.37
  568.8 156.8 %all-to-all-start.1 = ((bf16[16,96,2048]{2,1,0:T(8,128)(2,1)}), bf16[16,96,2048]{2,1,0:T(8,128)(2,1)}, u32[]{:S(2)}, u32[]{:S(2)}) async-start(bf16[16,96,2048]{2,1,0:T(8,128)(2,1)} %bitcast.294), calls=%async_computation.2 | async-start | bytes 12582912 | tf_op jit(solution)/shard_map/all_to_all | solution.py:214
  573.9 12.5 copy-start.34
  573.9 12.5 copy-start.38
  725.6 156.4 %all-to-all-start.3 = ((bf16[16,96,2048]{2,1,0:T(8,128)(2,1)}), bf16[16,96,2048]{2,1,0:T(8,128)(2,1)}, u32[]{:S(2)}, u32[]{:S(2)}) async-start(bf16[16,96,2048]{2,1,0:T(8,128)(2,1)} %bitcast.293), calls=%async_computation.4 | async-start | bytes 12582912 | tf_op jit(solution)/shard_map/all_to_all | solution.py:253
  730.3 215.2 %all-gather.11.cloned.1.call-start = ((), (), s32[]{:S(2)}) async-start(), calls=%async_computation.15 | async-start | bytes 2621440 | tf_op jit(solution)/shard_map/all_gather | solution.py:295
  894.4 5.2 copy-start.7
  894.4 8.1 copy-start.5
  901.6 1.0 copy-start.9
  903.8 188.9 %reduce-scatter.10.cloned.1.call-start = ((), (), s32[]{:S(2)}) async-start(), calls=%async_computation.16 | async-start | bytes 2621440 | tf_op jit(solution)/shard_map/reduce_scatter | solution.py:376
  1054.1 72.9 %reduce-scatter.12.cloned.1.call-start = ((), (), s32[]{:S(2)}) async-start(), calls=%async_computation.17 | async-start | bytes 2621440 | tf_op jit(solution)/shard_map/reduce_scatter | solution.py:382
  1057.9 87.4 %reduce-scatter.20.cloned.1.call-start = ((), (), s32[]{:S(2)}) async-start(), calls=%async_computation.22 | async-start | bytes 6291456 | tf_op jit(solution)/shard_map/reduce_scatter | solution.py:271
  1069.7 88.5 %reduce-scatter.18.cloned.1.call-start = ((), (), s32[]{:S(2)}) async-start(), calls=%async_computation.21 | async-start | bytes 6291456 | tf_op jit(solution)/shard_map/reduce_scatter | solution.py:268
  1081.0 93.2 %reduce-scatter.16.cloned.1.call-start = ((), (), s32[]{:S(2)}) async-start(), calls=%async_computation.20 | async-start | bytes 6291456 | tf_op jit(solution)/shard_map/reduce_scatter | solution.py:265
  1092.3 1.8 copy-start.12
  1092.3 1.8 copy-start.14
  1092.3 3.6 copy-start.3
  1092.3 3.6 copy-start.18
  1092.3 3.6 copy-start.26
  1092.3 129.8 %reduce-scatter.14.cloned.1.call-start = ((), (), s32[]{:S(2)}) async-start(), calls=%async_computation.18 | async-start | bytes 2621440 | tf_op jit(solution)/shard_map/reduce_scatter | solution.py:395
  1095.8 0.7 copy-start.23
  1127.0 7.9 copy-start.16
  1134.8 5.0 copy-start.36
  1134.8 216.9 %all-reduce.9.cloned.1.call-start = ((), (), s32[]{:S(2)}) async-start(), calls=%async_computation.23 | async-start | bytes 16777216 | tf_op jit(solution)/shard_map/psum | solution.py:407
  1134.9 4.9 copy-start.35
  1145.2 337.2 %all-reduce.7.cloned.1.call-start = ((), (), s32[]{:S(2)}) async-start(), calls=%async_computation.19 | async-start | bytes 262144 | tf_op jit(solution)/shard_map/psum | solution.py:411
  1162.3 16.1 %copy-start.8 = (bf16[128,2048]{1,0:T(8,128)(2,1)S(1)}, bf16[128,2048]{1,0:T(8,128)(2,1)}, u32[]{:S(2)}) copy-start(bf16[128,2048]{1,0:T(8,128)(2,1)} %reduce-scatter.8.cloned.1.call-done) | copy-start | bytes 1572868
  1162.3 59.8 %copy-start.21 = (f32[2048]{0:T(1024)S(1)}, f32[2048]{0:T(1024)}, u32[]{:S(2)}) copy-start(f32[2048]{0:T(1024)} %param.29) | copy-start | bytes 24580
  1162.3 59.8 %copy-start.29 = (f32[128]{0:T(128)S(1)}, f32[128]{0:T(128)}, u32[]{:S(2)}) copy-start(f32[128]{0:T(128)} %copy-done.28) | copy-start | bytes 1540
  1162.3 61.4 %copy-start.31 = (f32[128]{0:T(128)S(1)}, f32[128]{0:T(128)}, u32[]{:S(2)}) copy-start(f32[128]{0:T(128)} %copy-done.30) | copy-start | bytes 1540
  1162.3 61.5 %copy-start.6 = (f32[1,128,2048]{2,1,0:T(8,128)S(1)}, f32[1,128,2048]{2,1,0:T(8,128)}, u32[]{:S(2)}) copy-start(f32[1,128,2048]{2,1,0:T(8,128)} %param.39) | copy-start | bytes 3145732
  1162.3 61.5 %copy-start.10 = (f32[128,2048]{1,0:T(8,128)S(1)}, f32[128,2048]{1,0:T(8,128)}, u32[]{:S(2)}) copy-start(f32[128,2048]{1,0:T(8,128)} %copy-done.9) | copy-start | bytes 3145732
  1355.8 9.6 copy-start.27
  1355.8 128.2 %copy-start.1 = (bf16[512,2048]{1,0:T(8,128)(2,1)S(1)}, bf16[512,2048]{1,0:T(8,128)(2,1)}, u32[]{:S(2)}) copy-start(bf16[512,2048]{1,0:T(8,128)(2,1)} %param.32) | copy-start | bytes 6291460
Sparse Core Ops, SparseCore 0:
  10.8 48.3 all-gather.4
  66.6 33.8 all-gather.8
  102.9 35.1 all-gather.6
  173.9 43.6 reduce-scatter.7
  903.9 41.5 all-gather.10
  1054.2 33.9 reduce-scatter.9
  1091.8 35.1 reduce-scatter.11
  1129.9 12.0 reduce-scatter.19
  1144.8 13.3 reduce-scatter.17
  1160.9 13.3 reduce-scatter.15
  1177.1 44.9 reduce-scatter.13
  1226.3 125.3 all-reduce.8
  1357.8 124.5 all-reduce.6
where the time goes:
time: 1500 us; the launch traced here: 1490 us
  waiting for transfers between devices  968 us (65%)
  matrix products  243 us (16%)
  local copies, waits for them, and re-layouts  87.3 us (6%)
  other arithmetic  79.3 us (5%)
  blocking collectives  54.3 us (4%)
  loops' own time  23.1 us (2%)
  starting transfers between devices  20.9 us (1%)
  between operations  15 us (1%)
    all_to_all x1, waiting for transfers between devices, on_device(): lax.all_to_all(sending, ('context', 'expert'), split_axis=0, concat_axis=...  136 us
    all_to_all x1, waiting for transfers between devices, on_device(): lax.all_to_all(grad_rows.reshape(grad_arrived.shape), ('context', 'expert...  133 us
    all_to_all x1, waiting for transfers between devices, on_device(): lax.all_to_all(grad_sending, ('context', 'expert'), split_axis=0, concat_...  129 us
    all_to_all x1, waiting for transfers between devices, on_device(): lax.all_to_all(result, ('context', 'expert'), split_axis=0, concat_axis=0...  128 us
    psum x1, waiting for transfers between devices, on_device(): lax.psum(qkv_grad.astype(jnp.bfloat16), ('dp', 'context'))  125 us
    dot_general x8, matrix products, contract(): lax.dot_general(left, right, (((left_dim,), (right_dim,)), ((), ())), pre...  84.1 us
    psum x1, waiting for transfers between devices, on_device(): lax.psum((attn_gain_part, moe_gain_part, router_part), ('dp', 'context',...  77.4 us
    all_gather x1, waiting for transfers between devices, on_device(): gathered_in = lax.all_gather(normed_b, 'expert', axis=0, tiled=True)  47.2 us
  transfers between devices with their start and end apart: 17, of which 15 were waited for; matrix products, arithmetic and copies ran while one was open for 14% of the time, Pallas kernels for 0%

commit v1 on v0

--- a/solution.py
+++ b/solution.py
@@ -1,6 +1,10 @@
+import functools
+
 import jax
 import jax.numpy as jnp
 from jax import lax
+from jax.experimental import pallas as pl
+from jax.experimental.pallas import tpu as pltpu
 from jax.sharding import PartitionSpec as P
 
 HEAD_DIM = 128
@@ -61,7 +65,364 @@
     )
 
 
-def on_device(
+def nt_dot(left, right):
+    return lax.dot_general(
+        left, right, (((1,), (1,)), ((), ())), preferred_element_type=jnp.float32
+    )
+
+
+def tn_dot(left, right):
+    return lax.dot_general(
+        left, right, (((0,), (0,)), ((), ())), preferred_element_type=jnp.float32
+    )
+
+
+def nn_dot(left, right):
+    return jnp.dot(left, right, preferred_element_type=jnp.float32)
+
+
+def as_row(column):
+    wide = jnp.broadcast_to(column, (column.shape[0], 128))
+    return jnp.transpose(wide)[0:1]
+
+
+def piece_start(piece, blocks, half):
+    return jnp.where(
+        piece < blocks, piece * 2 * half, (2 * blocks - 1 - piece) * 2 * half + half
+    )
+
+
+def attend_kernel(blocks, half, place_ref, q_ref, k_ref, v_ref, out_ref, lse_ref):
+    mine = place_ref[0]
+    scale = HEAD_DIM ** (-0.5)
+    row_ids = lax.broadcasted_iota(jnp.int32, (half, half), 0)
+    col_ids = lax.broadcasted_iota(jnp.int32, (half, half), 1)
+    for part in range(2):
+        own = mine if part == 0 else 2 * blocks - 1 - mine
+        rows = pl.ds(part * half, half)
+        queries = q_ref[rows, :]
+
+        def tile(piece):
+            start = pl.multiple_of(piece_start(piece, blocks, half), half)
+            scores = nt_dot(queries, k_ref[pl.ds(start, half), :]) * scale
+            return jnp.exp(scores), v_ref[pl.ds(start, half), :]
+
+        def step(piece, carry):
+            total, acc = carry
+            prob, value = tile(piece)
+            total = total + jnp.sum(prob, axis=-1, keepdims=True)
+            return total, acc + nn_dot(prob.astype(jnp.bfloat16), value)
+
+        total, acc = lax.fori_loop(
+            0,
+            own,
+            step,
+            (jnp.zeros((half, 1), jnp.float32), jnp.zeros((half, HEAD_DIM), jnp.float32)),
+        )
+        prob, value = tile(own)
+        prob = jnp.where(col_ids <= row_ids, prob, 0.0)
+        total = total + jnp.sum(prob, axis=-1, keepdims=True)
+        acc = acc + nn_dot(prob.astype(jnp.bfloat16), value)
+        out_ref[rows, :] = (acc / total).astype(jnp.bfloat16)
+        lse_ref[0, :, pl.ds(part * half, half)] = as_row(jnp.log(total))
+
+
+def attend(place, queries, keys, values, blocks):
+    span, feat = queries.shape
+    seq = keys.shape[0]
+    heads = feat // HEAD_DIM
+    half = span // 2
+    head_block = lambda rows: pl.BlockSpec((rows, HEAD_DIM), lambda h: (0, h))
+    return pl.pallas_call(
+        functools.partial(attend_kernel, blocks, half),
+        grid=(heads,),
+        in_specs=[
+            pl.BlockSpec(memory_space=pltpu.SMEM),
+            head_block(span),
+            head_block(seq),
+            head_block(seq),
+        ],
+        out_specs=[head_block(span), pl.BlockSpec((1, 1, span), lambda h: (h, 0, 0))],
+        out_shape=[
+            jax.ShapeDtypeStruct((span, feat), jnp.bfloat16),
+            jax.ShapeDtypeStruct((heads, 1, span), jnp.float32),
+        ],
+        name="attend",
+    )(place, queries, keys, values)
+
+
+def attend_back_kernel(
+    blocks, half, place_ref, q_ref, g_ref, o_ref, lse_ref, k_ref, v_ref,
+    dq_ref, dk_ref, dv_ref, dk_acc, dv_acc,
+):
+    mine = place_ref[0]
+    scale = HEAD_DIM ** (-0.5)
+    key_ids = lax.broadcasted_iota(jnp.int32, (half, half), 0)
+    query_ids = lax.broadcasted_iota(jnp.int32, (half, half), 1)
+    dk_acc[...] = jnp.zeros_like(dk_acc)
+    dv_acc[...] = jnp.zeros_like(dv_acc)
+    for part in range(2):
+        own = mine if part == 0 else 2 * blocks - 1 - mine
+        rows = pl.ds(part * half, half)
+        queries = q_ref[rows, :]
+        grads = g_ref[rows, :]
+        lse = lse_ref[0, :, pl.ds(part * half, half)]
+        row_dot = as_row(
+            jnp.sum(
+                grads.astype(jnp.float32) * o_ref[rows, :].astype(jnp.float32),
+                axis=-1,
+                keepdims=True,
+            )
+        )
+
+        def tile(piece, masked, acc):
+            start = pl.multiple_of(piece_start(piece, blocks, half), half)
+            place = pl.ds(start, half)
+            keys = k_ref[place, :]
+            prob = jnp.exp(nt_dot(keys, queries) * scale - lse)
+            if masked:
+                prob = jnp.where(key_ids <= query_ids, prob, 0.0)
+            d_prob = nt_dot(v_ref[place, :], grads)
+            d_score = (prob * (d_prob - row_dot) * scale).astype(jnp.bfloat16)
+            dv_acc[place, :] += nn_dot(prob.astype(jnp.bfloat16), grads)
+            dk_acc[place, :] += nn_dot(d_score, queries)
+            return acc + tn_dot(d_score, keys)
+
+        acc = lax.fori_loop(
+            0,
+            own,
+            lambda piece, acc: tile(piece, False, acc),
+            jnp.zeros((half, HEAD_DIM), jnp.float32),
+        )
+        dq_ref[rows, :] = tile(own, True, acc)
+    dk_ref[...] = dk_acc[...].astype(jnp.bfloat16)
+    dv_ref[...] = dv_acc[...].astype(jnp.bfloat16)
+
+
+def attend_back(place, queries, grads, attended, lse, keys, values, blocks):
+    span, feat = queries.shape
+    seq = keys.shape[0]
+    heads = feat // HEAD_DIM
+    half = span // 2
+    head_block = lambda rows: pl.BlockSpec((rows, HEAD_DIM), lambda h: (0, h))
+    return pl.pallas_call(
+        functools.partial(attend_back_kernel, blocks, half),
+        grid=(heads,),
+        in_specs=[
+            pl.BlockSpec(memory_space=pltpu.SMEM),
+            head_block(span),
+            head_block(span),
+            head_block(span),
+            pl.BlockSpec((1, 1, span), lambda h: (h, 0, 0)),
+            head_block(seq),
+            head_block(seq),
+        ],
+        out_specs=[head_block(span), head_block(seq), head_block(seq)],
+        out_shape=[
+            jax.ShapeDtypeStruct((span, feat), jnp.float32),
+            jax.ShapeDtypeStruct((seq, feat), jnp.bfloat16),
+            jax.ShapeDtypeStruct((seq, feat), jnp.bfloat16),
+        ],
+        scratch_shapes=[pltpu.VMEM((seq, HEAD_DIM), jnp.float32)] * 2,
+        name="attend_back",
+    )(place, queries, grads, attended, lse, keys, values)
+
+
+def split_pair(values):
+    upper = values.astype(jnp.bfloat16)
+    lower = (values - upper.astype(jnp.float32)).astype(jnp.bfloat16)
+    return upper, lower
+
+
+TOKEN_AXES = ("context", "expert")
+
+
+def fast_device(
+    hidden_in,
+    attn_gain,
+    w_qkv,
+    qk_gain,
+    w_out,
+    moe_gain,
+    router,
+    w_gate,
+    w_up,
+    w_down,
+    expert_ids,
+    grad_out,
+):
+    tokens = hidden_in[0].astype(jnp.float32)
+    upstream = grad_out[0]
+    tok_count, model_width = tokens.shape
+    context_size = lax.axis_size("context")
+    expert_size = lax.axis_size("expert")
+    expert_count = router.shape[1]
+    span_rows = tok_count * expert_size
+    context_index = lax.axis_index("context")
+    own_expert = context_index * expert_size + lax.axis_index("expert")
+    place = jnp.full((1,), context_index, jnp.int32)
+    local_places = folded_positions(
+        context_index * span_rows + jnp.arange(span_rows, dtype=jnp.int32), span_rows, context_size
+    )
+
+    normed_b = rms_scale(tokens, attn_gain).astype(jnp.bfloat16)
+    gathered_in = lax.all_gather(normed_b, "expert", axis=0, tiled=True)
+    all_upstream = lax.all_gather(
+        upstream.astype(jnp.bfloat16), TOKEN_AXES, axis=0, tiled=True
+    )
+    projected = jnp.einsum(
+        "rd,kdf->krf", gathered_in, w_qkv[:2], preferred_element_type=jnp.float32
+    )
+    value_local = nn_dot(gathered_in, w_qkv[2]).astype(jnp.bfloat16)
+
+    def prep_local(pair_qk, gain_vec):
+        return qk_prep(pair_qk, gain_vec, local_places)
+
+    rotated = prep_local(projected, qk_gain).astype(jnp.bfloat16)
+    feat_width = projected.shape[2]
+    keys_all = lax.all_gather(rotated[1], "context", axis=0, tiled=True)
+    values_all = lax.all_gather(value_local, "context", axis=0, tiled=True)
+    attended, lse = attend(place, rotated[0], keys_all, values_all, context_size)
+    branch_out = lax.psum_scatter(
+        nn_dot(attended, w_out).astype(jnp.bfloat16), "expert", scatter_dimension=0, tiled=True
+    ).astype(jnp.float32)
+    resid = tokens + branch_out
+    mixed_in = rms_scale(resid, moe_gain)
+    logits = jnp.dot(
+        mixed_in, router, precision=lax.Precision.HIGHEST, preferred_element_type=jnp.float32
+    )
+    gate_probs = jax.nn.softmax(logits, axis=-1)
+    chosen = expert_ids[0]
+    picked = jnp.any(
+        chosen[:, :, None] == jnp.arange(expert_count, dtype=jnp.int32)[None, None, :], axis=1
+    )
+    weights = jnp.where(picked, gate_probs, 0.0)
+    expert_in = mixed_in.astype(jnp.bfloat16)
+    pad = jnp.zeros((tok_count, 128 - 2 * expert_count), jnp.bfloat16)
+    sending = jnp.concatenate([expert_in, *split_pair(weights), pad], axis=1)
+    arrived = lax.all_gather(sending, TOKEN_AXES, axis=0, tiled=True)
+    rows = arrived[:, :model_width]
+    pairs = arrived[:, model_width:].astype(jnp.float32)
+    lane = jnp.arange(128, dtype=jnp.int32)[None, :]
+    mine = (lane == own_expert) | (lane == own_expert + expert_count)
+    factor = jnp.sum(jnp.where(mine, pairs, 0.0), axis=1, keepdims=True)
+    gate_pre = nn_dot(rows, w_gate[0])
+    up_pre = nn_dot(rows, w_up[0])
+    back_hidden = nt_dot(all_upstream, w_down[0])
+    sigmoid_g = jax.nn.sigmoid(gate_pre)
+    activated = gate_pre * sigmoid_g
+    hidden = activated * up_pre
+    d_weight = jnp.sum(hidden * back_hidden, axis=1, keepdims=True)
+    hidden_w = (factor * hidden).astype(jnp.bfloat16)
+    grad_hidden = factor * back_hidden
+    grad_gate = (grad_hidden * up_pre * sigmoid_g * (1.0 + gate_pre * (1.0 - sigmoid_g))).astype(
+        jnp.bfloat16
+    )
+    grad_up = (grad_hidden * activated).astype(jnp.bfloat16)
+    grad_rows = (nt_dot(grad_gate, w_gate[0]) + nt_dot(grad_up, w_up[0])).astype(jnp.bfloat16)
+    upper, lower = split_pair(d_weight)
+    d_pairs = jnp.where(lane == own_expert, upper, jnp.zeros((), jnp.bfloat16)) + jnp.where(
+        lane == own_expert + expert_count, lower, jnp.zeros((), jnp.bfloat16)
+    )
+    returned = lax.psum_scatter(
+        jnp.concatenate([grad_rows, d_pairs], axis=1),
+        TOKEN_AXES,
+        scatter_dimension=0,
+        tiled=True,
+    ).astype(jnp.float32)
+    hidden_out = resid + lax.psum_scatter(
+        nn_dot(hidden_w, w_down[0]).astype(jnp.bfloat16),
+        TOKEN_AXES,
+        scatter_dimension=0,
+        tiled=True,
+    ).astype(jnp.float32)
+
+    def over_sequences(grad):
+        return lax.psum_scatter(
+            grad.astype(jnp.bfloat16)[None], "dp", scatter_dimension=1, tiled=True
+        ).astype(jnp.float32)
+
+    gate_sum = over_sequences(tn_dot(rows, grad_gate))
+    up_sum = over_sequences(tn_dot(rows, grad_up))
+    down_sum = over_sequences(tn_dot(hidden_w, all_upstream))
+
+    d_weights = (
+        returned[:, model_width : model_width + expert_count]
+        + returned[:, model_width + expert_count : model_width + 2 * expert_count]
+    )
+    d_gates = jnp.where(picked, d_weights, 0.0)
+    d_logits = gate_probs * (d_gates - jnp.sum(gate_probs * d_gates, axis=-1, keepdims=True))
+    router_part = lax.dot_general(
+        mixed_in,
+        d_logits,
+        (((0,), (0,)), ((), ())),
+        precision=lax.Precision.HIGHEST,
+        preferred_element_type=jnp.float32,
+    )
+    d_mixed = returned[:, :model_width] + lax.dot_general(
+        d_logits,
+        router,
+        (((1,), (1,)), ((), ())),
+        precision=lax.Precision.HIGHEST,
+        preferred_element_type=jnp.float32,
+    )
+    _, second_pull = jax.vjp(rms_scale, resid, moe_gain)
+    resid_part, moe_gain_part = second_pull(d_mixed)
+    d_resid = upstream + resid_part
+    grad_gathered = lax.all_gather(
+        d_resid.astype(jnp.bfloat16), "expert", axis=0, tiled=True
+    )
+    out_grad = tn_dot(attended, grad_gathered)
+    d_attended = nt_dot(grad_gathered, w_out).astype(jnp.bfloat16)
+    d_queries, key_part, value_part = attend_back(
+        place, rotated[0], d_attended, attended, lse, keys_all, values_all, context_size
+    )
+    key_grad = lax.psum_scatter(
+        key_part, "context", scatter_dimension=0, tiled=True
+    ).astype(jnp.float32)
+    value_grad = lax.psum_scatter(
+        value_part, "context", scatter_dimension=0, tiled=True
+    ).astype(jnp.float32)
+    d_rotated = jnp.stack([d_queries, key_grad])
+    _, prep_pull = jax.vjp(prep_local, projected, qk_gain)
+    d_pair, qk_part = prep_pull(d_rotated)
+    d_proj = jnp.concatenate([d_pair, value_grad[None]], axis=0).astype(jnp.bfloat16)
+    qkv_grad = jnp.einsum("rd,krf->kdf", gathered_in, d_proj, preferred_element_type=jnp.float32)
+    d_normed = lax.psum_scatter(
+        jnp.einsum("krf,kdf->rd", d_proj, w_qkv, preferred_element_type=jnp.float32).astype(
+            jnp.bfloat16
+        ),
+        "expert",
+        scatter_dimension=0,
+        tiled=True,
+    ).astype(jnp.float32)
+    _, first_pull = jax.vjp(rms_scale, tokens, attn_gain)
+    token_part, attn_gain_part = first_pull(d_normed)
+    grad_in = d_resid + token_part
+    qkv_sum, out_sum, qk_sum = (
+        lax.psum(qkv_grad.astype(jnp.bfloat16), ("dp", "context")).astype(jnp.float32),
+        lax.psum(out_grad.astype(jnp.bfloat16), ("dp", "context")).astype(jnp.float32),
+        lax.psum(qk_part.astype(jnp.bfloat16), ("dp", "context")).astype(jnp.float32),
+    )
+    attn_sum, moe_sum, router_sum = lax.psum(
+        (attn_gain_part, moe_gain_part, router_part), ("dp", "context", "expert")
+    )
+    return (
+        hidden_out[None],
+        grad_in[None],
+        attn_sum,
+        qkv_sum,
+        qk_sum,
+        out_sum,
+        moe_sum,
+        router_sum,
+        gate_sum,
+        up_sum,
+        down_sum,
+    )
+
+
+def portable_device(
     hidden_in,
     attn_gain,
     w_qkv,
@@ -427,6 +788,8 @@
 
 
 def solution(mesh):
+    grouped = mesh.shape["context"] == 4 and mesh.shape["expert"] == 4
+    on_device = fast_device if grouped else portable_device
     placed = (
         P("dp", ("context", "expert"), None),
         P(),

time: 1500 us -> 1300 us (0.87)
  matrix products: 243 us -> 179 us
  waiting for transfers between devices: 968 us -> 907 us
  other arithmetic: 79.3 us -> 42.2 us
  Pallas kernels: 0 us -> 36.7 us
  local copies, waits for them, and re-layouts: 87.3 us -> 51.7 us
  loops' own time: 23.1 us -> 0 us
  starting transfers between devices: 20.9 us -> 0.89 us
    all_to_all x4 -> x0, waiting for transfers between devices: 526 us -> none  [the longest x1 136 us: on_device(): lax.all_to_all(sending, ('context', 'expert'), split_axis=0, concat_axis=...]
    unnamed x13 -> x21, waiting for transfers between devices: 0.21 us -> 437 us
    all_gather x4 -> x6, waiting for transfers between devices: 126 us -> 403 us  [the longest x1 135 us: fast_device(): arrived = lax.all_gather(sending, TOKEN_AXES, axis=0, tiled=True)]
    psum x2, waiting for transfers between devices: 202 us -> 43.3 us  [the longest x1 43.3 us: fast_device(): lax.psum((attn_gain_part, moe_gain_part, router_part), ('dp', 'context',...]
    reduce_scatter x7 -> x5, waiting for transfers between devices: 113 us -> 23 us  [the longest x3 19.7 us: over_sequences(): lax.psum_scatter(grad.astype(jnp.bfloat16)[None], 'dp', scatter_dimension...]
    dot_general x55 -> x19, matrix products: 243 us -> 179 us  [the longest x5 60.6 us: nn_dot(): return jnp.dot(left, right, preferred_element_type=jnp.float32)]
    pallas_call x0 -> x2, Pallas kernels: none -> 36.7 us  [the longest x1 21.9 us: attend_back(): pl.pallas_call(functools.partial(attend_back_kernel, blocks, half), grid=...]
    gather x2 -> x0, local copies, waits for them, and re-layouts: 24.8 us -> none  [the longest x1 12.4 us: on_device(): dispatched.reshape(expert_count * capacity, model_width)[target]]
  transfers between devices with their start and end apart: 17 -> 17, of which waited for: 15 -> 14; matrix products, arithmetic and copies ran while one was open for 14% -> 13% of each run, Pallas kernels for 0% -> 0%
where the time goes in v1:
time: 1300 us; the launch traced here: 1290 us
  waiting for transfers between devices  907 us (70%)
  matrix products  179 us (14%)
  blocking collectives  52.5 us (4%)
  local copies, waits for them, and re-layouts  51.7 us (4%)
  other arithmetic  42.2 us (3%)
  Pallas kernels  36.7 us (3%)
  between operations  16.8 us (1%)
    unnamed x21, waiting for transfers between devices  437 us
    all_gather x1, waiting for transfers between devices, fast_device(): arrived = lax.all_gather(sending, TOKEN_AXES, axis=0, tiled=True)  135 us
    all_gather x1, waiting for transfers between devices, fast_device(): lax.all_gather(upstream.astype(jnp.bfloat16), TOKEN_AXES, axis=0, tiled=T...  113 us
    dot_general x5, matrix products, nn_dot(): return jnp.dot(left, right, preferred_element_type=jnp.float32)  60.6 us
    all_gather x1, waiting for transfers between devices, fast_device(): gathered_in = lax.all_gather(normed_b, 'expert', axis=0, tiled=True)  49.1 us
    dot_general x4, matrix products, nt_dot(): lax.dot_general(left, right, (((1,), (1,)), ((), ())), preferred_element_...  47.9 us
    dot_general x4, matrix products, tn_dot(): lax.dot_general(left, right, (((0,), (0,)), ((), ())), preferred_element_...  46.5 us
    all_gather x1, waiting for transfers between devices, fast_device(): lax.all_gather(d_resid.astype(jnp.bfloat16), 'expert', axis=0, tiled=True)  46 us
  transfers between devices with their start and end apart: 17, of which 14 were waited for; matrix products, arithmetic and copies ran while one was open for 13% of the time, Pallas kernels for 0%

profile of v1, /device:TPU:0, one launch (start us, length us, event | category | flops | bytes accessed | tf_op | source)
XLA Modules:
  0.0 1286.5 jit_solution(2191734127990829553)
XLA Ops:
  8.1 1.4 copy.76
  10.9 1.8 fusion.34
  12.8 49.1 %all-gather.7.cloned.1.call-done = bf16[512,2048]{0,1:T(8,128)(2,1)} async-done(((bf16[128,2048]{0,1:T(8,128)(2,1)}), bf16[512,2048]{0,1:T(8,128)(2,1)}) %all-gather.7.cloned.1.call-update) | async-done | bytes 2097168 | tf_op jit(solution)/shard_map/all_gather | solution.py:269
  61.9 4.3 fusion.29
  66.9 5.3 multiply_reduce_fusion.3
  74.2 2.0 copy.100
  77.3 22.4 %all-gather.11.cloned.1.call-done.v_ref = bf16[2048,512]{1,0:T(8,128)(2,1)} async-done(((bf16[512,512]{1,0:T(8,128)(2,1)}), bf16[2048,512]{1,0:T(8,128)(2,1)}) %all-gather.11.cloned.1.call-update) | async-done | bytes 2097168 | tf_op jit(solution)/shard_map/all_gather | solution.py:284
  99.8 37.6 %all-gather.9.cloned.1.call-done.k_ref = bf16[2048,512]{1,0:T(8,128)(2,1)} async-done(((bf16[512,512]{1,0:T(8,128)(2,1)}), bf16[2048,512]{1,0:T(8,128)(2,1)}) %all-gather.9.cloned.1.call-update) | async-done | bytes 2097168 | tf_op jit(solution)/shard_map/all_gather | solution.py:283
  137.4 14.8 %attend.1 = (bf16[512,512]{1,0:T(8,128)(2,1)}, f32[4,1,512]{2,1,0:T(1,128)}) custom-call(s32[1]{0:T(128)} %bitcast.1.place_ref, bf16[512,512]{1,0:T(8,128)(2,1)} %copy.99.q_ref, bf16[2048,512]{1,0:T(8,128)(2,1)} %all-gather.9.cloned.1.call-done.k_ref, bf16[2048,512]{1,0:T(8,128)(2,1)} %all-gather.11.cloned.1.call-done.v_ref), custom_call_target="tpu_custom_call" | custom-call | tf_op jit(solution)/shard_map/attend/pallas_call | solution.py:136
  152.2 3.6 convolution_convert_fusion.2
  155.9 2.6 copy.83
  158.4 2.1 bitcast_convert_fusion.1
  160.7 39.0 %reduce-scatter.28.cloned.1.call-done = bf16[128,2048]{1,0:T(8,128)(2,1)} async-done(((bf16[512,2048]{1,0:T(8,128)(2,1)}), bf16[128,2048]{1,0:T(8,128)(2,1)}) %reduce-scatter.28.cloned.1.call-update) | async-done | bytes 524304
  199.7 1.3 copy.106
  204.0 112.7 %all-gather.15.cloned.1.call-done = bf16[2048,2048]{0,1:T(8,128)(2,1)} async-done(((bf16[128,2048]{0,1:T(8,128)(2,1)}), bf16[2048,2048]{0,1:T(8,128)(2,1)}) %all-gather.15.cloned.1.call-update) | async-done | bytes 8388624 | tf_op jit(solution)/shard_map/all_gather | solution.py:270
  316.7 14.4 %fusion.9 = f32[2048,1024]{0,1:T(8,128)} fusion(bf16[2048,2048]{0,1:T(8,128)(2,1)} %all-gather.15.cloned.1.call-done, bf16[1,1024,2048]{2,1,0:T(8,128)(2,1)} %param.21), kind=kOutput, calls=%fused_computation.19 | convolution fusion | flops 8589934592 | bytes 20971520 | tf_op jit(solution)/shard_map/dot_general | solution.py:69
  331.2 135.3 %all-gather.13.cloned.1.call-done = bf16[2048,2176]{0,1:T(8,128)(2,1)} async-done(((bf16[128,2176]{0,1:T(8,128)(2,1)}), bf16[2048,2176]{0,1:T(8,128)(2,1)}) %all-gather.13.cloned.1.call-update) | async-done | bytes 8912912 | tf_op jit(solution)/shard_map/all_gather | solution.py:303
  466.4 1.2 select_reduce_fusion
  467.7 14.6 %fusion.5 = f32[2048,1024]{0,1:T(8,128)} fusion(bf16[2048,2176]{0,1:T(8,128)(2,1)} %all-gather.13.cloned.1.call-done, bf16[1,2048,1024]{2,1,0:T(8,128)(2,1)} %param.20), kind=kOutput, calls=%fused_computation.14 | convolution fusion | flops 8589934592 | bytes 20971520 | tf_op jit(solution)/shard_map/dot_general | solution.py:81
  482.3 23.8 %multiply_convert_fusion.1 = (bf16[2048,1024]{0,1:T(8,128)(2,1)}, f32[2048]{0:T(1024)S(1)}, bf16[2048,1024]{0,1:T(8,128)(2,1)}, bf16[2048,1024]{0,1:T(8,128)(2,1)}) fusion(f32[2048,1024]{0,1:T(8,128)} %fusion.5, f32[2048,1024]{0,1:T(8,128)} %fusion.9, f32[2048]{0:T(1024)S(1)} %select_reduce_fusion, bf16[1,2048,1024]{2,1,0:T(8,128)(2,1)} %param.19, ...), kind=kOutput, calls=%fused_computation.4 | convolution fusion | flops 8629778432 | bytes 41959424 | tf_op jit(solution)/shard_map/dot_general | solution.py:81
  506.1 15.1 %fusion.14 = f32[2048,2048]{0,1:T(8,128)} fusion(bf16[2048,1024]{0,1:T(8,128)(2,1)} %get-tuple-element.90, bf16[1,2048,1024]{2,1,0:T(8,128)(2,1)} %param.19), kind=kOutput, calls=%fused_computation.24 | convolution fusion | flops 8589934592 | bytes 25165824 | tf_op jit(solution)/shard_map/dot_general | solution.py:69
  521.2 14.7 %add_convert_fusion = bf16[2048,2048]{0,1:T(8,128)(2,1)S(1)} fusion(f32[2048,2048]{0,1:T(8,128)} %fusion.14, bf16[2048,1024]{0,1:T(8,128)(2,1)} %get-tuple-element.92, bf16[1,2048,1024]{2,1,0:T(8,128)(2,1)} %param.20), kind=kOutput, calls=%fused_computation | convolution fusion | flops 8598323200 | bytes 33554432 | tf_op jit(solution)/shard_map/dot_general | solution.py:69
  536.1 4.2 pad_maximum_fusion
  540.3 11.8 copy.109
  552.1 189.0 %reduce-scatter.32.cloned.1.call-done = bf16[128,2176]{1,0:T(8,128)(2,1)} async-done(((bf16[2048,2176]{1,0:T(8,128)(2,1)}), bf16[128,2176]{1,0:T(8,128)(2,1)}) %reduce-scatter.32.cloned.1.call-update) | async-done | bytes 557072
  741.1 2.1 copy.110
  743.2 1.2 convert_element_type.173
  744.4 2.3 multiply_reduce_fusion.4
  749.1 46.0 %all-gather.17.cloned.1.call-done = bf16[512,2048]{0,1:T(8,128)(2,1)} async-done(((bf16[128,2048]{0,1:T(8,128)(2,1)}), bf16[512,2048]{0,1:T(8,128)(2,1)}) %all-gather.17.cloned.1.call-update) | async-done | bytes 2097168 | tf_op jit(solution)/shard_map/all_gather | solution.py:372
  795.1 3.7 convolution_convert_fusion.3.g_ref
  798.8 21.9 %attend_back.1 = (f32[512,512]{1,0:T(8,128)}, bf16[2048,512]{1,0:T(8,128)(2,1)}, bf16[2048,512]{1,0:T(8,128)(2,1)}) custom-call(s32[1]{0:T(128)} %bitcast.1.place_ref, bf16[512,512]{1,0:T(8,128)(2,1)} %copy.99.q_ref, bf16[512,512]{1,0:T(8,128)(2,1)} %convolution_convert_fusion.3.g_ref, bf16[512,512]{1,0:T(8,128)(2,1)} %get-tuple-element.16.o_ref, ...), custom_call_target="tpu_custom_call" | custom-call | tf_op jit(solution)/shard_map/attend_back/pallas_call | solution.py:208
  821.5 14.1 %convert_bitcast_fusion.1 = bf16[1,1024,2048]{2,1,0:T(8,128)(2,1)} fusion(bf16[2048,1024]{0,1:T(8,128)(2,1)} %get-tuple-element.93, bf16[2048,2048]{0,1:T(8,128)(2,1)} %all-gather.15.cloned.1.call-done), kind=kOutput, calls=%fused_computation.27 | convolution fusion | flops 8592031744 | bytes 16777216 | tf_op jit(solution)/shard_map/dot_general | solution.py:75
  835.6 13.9 %convert_bitcast_fusion.3 = bf16[1,2048,1024]{2,1,0:T(8,128)(2,1)} fusion(bf16[2048,1024]{0,1:T(8,128)(2,1)} %get-tuple-element.90, bf16[2048,2176]{0,1:T(8,128)(2,1)} %all-gather.13.cloned.1.call-done), kind=kOutput, calls=%fused_computation.29 | convolution fusion | flops 8592031744 | bytes 16777216 | tf_op jit(solution)/shard_map/dot_general | solution.py:75
  849.7 14.0 %convert_bitcast_fusion.2 = bf16[1,2048,1024]{2,1,0:T(8,128)(2,1)} fusion(bf16[2048,1024]{0,1:T(8,128)(2,1)} %get-tuple-element.92, bf16[2048,2176]{0,1:T(8,128)(2,1)} %all-gather.13.cloned.1.call-done), kind=kOutput, calls=%fused_computation.28 | convolution fusion | flops 8592031744 | bytes 16777216 | tf_op jit(solution)/shard_map/dot_general | solution.py:75
  863.8 14.2 %convolution_convert_fusion = bf16[2048,2048]{1,0:T(8,128)(2,1)} fusion(bf16[2048,1024]{0,1:T(8,128)(2,1)} %get-tuple-element.93, bf16[1,1024,2048]{2,1,0:T(8,128)(2,1)} %param.21), kind=kOutput, calls=%fused_computation.8 | convolution fusion | flops 8594128896 | bytes 16777216 | tf_op jit(solution)/shard_map/dot_general | solution.py:81
  878.1 2.7 copy.101
  880.8 2.2 copy.102
  883.0 2.4 multiply_add_fusion.1
  886.2 1.4 fusion.23
  887.6 1.5 copy.103
  889.1 3.3 reduce-scatter.20.cloned.1.call-done
  892.4 7.8 bitcast_convert_fusion
  900.3 4.5 convolution_convert_fusion.1
  904.8 5.7 convert_bitcast_fusion
  910.6 4.1 convert_element_type.191
  914.7 8.4 reduce-scatter.22.cloned.1.call-done
  923.1 4.1 convert_element_type.187
  927.2 11.3 reduce-scatter.24.cloned.1.call-done
  938.5 4.1 convert_element_type.189
  942.6 180.4 %reduce-scatter.30.cloned.1.call-done = bf16[128,2048]{1,0:T(8,128)(2,1)} async-done(((bf16[2048,2048]{1,0:T(8,128)(2,1)}), bf16[128,2048]{1,0:T(8,128)(2,1)}) %reduce-scatter.30.cloned.1.call-update) | async-done | bytes 524304
  1123.0 2.1 copy.108
  1125.0 1.9 fusion.42
  1126.9 12.9 psum.44
  1140.4 28.2 %reduce-scatter.34.cloned.1.call-done = bf16[128,2048]{1,0:T(8,128)(2,1)} async-done(((bf16[512,2048]{1,0:T(8,128)(2,1)}), bf16[128,2048]{1,0:T(8,128)(2,1)}) %reduce-scatter.34.cloned.1.call-update) | async-done | bytes 524304
  1168.6 2.0 copy.112
  1170.7 1.8 fusion.35
  1172.5 2.7 fusion.38
  1175.2 2.5 copy.92
  1177.7 2.5 copy.91
  1180.3 4.1 convert_element_type.185
  1184.4 9.6 copy.93
  1194.0 39.6 %all-reduce.2 = (f32[2048]{0:T(1024)}, f32[2048]{0:T(1024)}) all-reduce(f32[2048]{0:T(1024)S(1)} %get-tuple-element.80, f32[2048]{0:T(1024)S(1)} %get-tuple-element.76), channel_id=1, replica_groups=mesh['dp'=2,'context'=4,'expert'=4] {'dp','context','expert'}, use_global_device_ids=true, to_apply=%region_19.20 | all-reduce | flops 4096 | bytes 32768 | tf_op jit(solution)/shard_map/psum | solution.py:407
  1233.6 43.3 %all-reduce.7.cloned.1.call-done = f32[2048,16]{0,1:T(8,128)} async-done(((f32[2048,16]{0,1:T(8,128)}), f32[2048,16]{0,1:T(8,128)}) %all-reduce.7.cloned.1.call-update) | async-done | bytes 131088 | tf_op jit(solution)/shard_map/psum | solution.py:407
  1276.9 1.6 copy.120
  (130 shorter events, 13.4 us)
Async XLA Ops:
  8.0 144.2 %copy-start = (bf16[512,2048]{1,0:T(8,128)(2,1)S(1)}, bf16[512,2048]{1,0:T(8,128)(2,1)}, u32[]{:S(2)}) copy-start(bf16[512,2048]{1,0:T(8,128)(2,1)} %param.16) | copy-start | bytes 6291460
  8.0 53.9 %all-gather.7.cloned.1.call-start = ((), (), s32[]{:S(2)}) async-start(), calls=%async_computation.9 | async-start | bytes 2621440 | tf_op jit(solution)/shard_map/all_gather | solution.py:269
  9.5 56.8 %copy-start.25 = (f32[2,512]{1,0:T(2,128)S(1)}, f32[2,512]{1,0:T(2,128)}, u32[]{:S(2)}) copy-start(f32[2,512]{1,0:T(2,128)} %param.15) | copy-start | bytes 12292
  9.8 0.5 copy-start.26
  10.4 0.6 copy-start.22
  12.8 87.0 %all-gather.11.cloned.1.call-start = ((), (), s32[]{:S(2)}) async-start(), calls=%async_computation.11 | async-start | bytes 2621440 | tf_op jit(solution)/shard_map/all_gather | solution.py:284
  66.3 71.1 %all-gather.9.cloned.1.call-start = ((), (), s32[]{:S(2)}) async-start(), calls=%async_computation.10 | async-start | bytes 2621440 | tf_op jit(solution)/shard_map/all_gather | solution.py:283
  66.3 6.0 copy-start.20
  66.9 6.1 copy-start.8
  66.9 6.0 copy-start.10
  72.3 2.0 copy-start.2
  72.3 1.9 copy-start.18
  72.3 0.7 copy-start.13
  76.3 123.4 %reduce-scatter.28.cloned.1.call-start = ((), (), s32[]{:S(2)}) async-start(), calls=%async_computation.21 | async-start | bytes 2621440
  155.8 4.9 copy-start.24
  155.8 45.5 %copy-start.15 = (f32[2048]{0:T(1024)S(1)}, f32[2048]{0:T(1024)}, u32[]{:S(2)}) copy-start(f32[2048]{0:T(1024)} %param.17) | copy-start | bytes 24580
  155.8 45.5 %copy-start.16 = (f32[2048,16]{0,1:T(8,128)S(1)}, f32[2048,16]{0,1:T(8,128)}, u32[]{:S(2)}) copy-start(f32[2048,16]{0,1:T(8,128)} %param.18) | copy-start | bytes 393220
  155.8 160.9 %all-gather.15.cloned.1.call-start = ((), (), s32[]{:S(2)}) async-start(), calls=%async_computation.13 | async-start | bytes 8912896 | tf_op jit(solution)/shard_map/all_gather | solution.py:270
  160.5 305.9 %all-gather.13.cloned.1.call-start = ((), (), s32[]{:S(2)}) async-start(), calls=%async_computation.12 | async-start | bytes 9469952 | tf_op jit(solution)/shard_map/all_gather | solution.py:303
  203.8 537.3 %reduce-scatter.32.cloned.1.call-start = ((), (), s32[]{:S(2)}) async-start(), calls=%async_computation.23 | async-start | bytes 9469952
  552.1 243.0 %all-gather.17.cloned.1.call-start = ((), (), s32[]{:S(2)}) async-start(), calls=%async_computation.14 | async-start | bytes 2621440 | tf_op jit(solution)/shard_map/all_gather | solution.py:372
  743.2 4.6 copy-start.4
  746.8 1.0 copy-start.6
  749.0 131.8 %reduce-scatter.18.cloned.1.call-start = ((), (), s32[]{:S(2)}) async-start(), calls=%async_computation.15 | async-start | bytes 2621440 | tf_op jit(solution)/shard_map/reduce_scatter | solution.py:380
  820.7 71.7 %reduce-scatter.20.cloned.1.call-start = ((), (), s32[]{:S(2)}) async-start(), calls=%async_computation.16 | async-start | bytes 2621440 | tf_op jit(solution)/shard_map/reduce_scatter | solution.py:383
  821.5 89.1 %reduce-scatter.26.cloned.1.call-start = ((), (), s32[]{:S(2)}) async-start(), calls=%async_computation.20 | async-start | bytes 6291456 | tf_op jit(solution)/shard_map/reduce_scatter | solution.py:341
  835.6 87.5 %reduce-scatter.22.cloned.1.call-start = ((), (), s32[]{:S(2)}) async-start(), calls=%async_computation.18 | async-start | bytes 6291456 | tf_op jit(solution)/shard_map/reduce_scatter | solution.py:341
  849.6 88.9 %reduce-scatter.24.cloned.1.call-start = ((), (), s32[]{:S(2)}) async-start(), calls=%async_computation.19 | async-start | bytes 6291456 | tf_op jit(solution)/shard_map/reduce_scatter | solution.py:341
  863.7 259.2 %reduce-scatter.30.cloned.1.call-start = ((), (), s32[]{:S(2)}) async-start(), calls=%async_computation.22 | async-start | bytes 8912896
  878.0 5.0 copy-start.9
  878.0 5.0 copy-start.11
  878.0 7.4 copy-start.3
  878.0 7.4 copy-start.14
  878.0 7.4 copy-start.21
  878.1 290.5 %reduce-scatter.34.cloned.1.call-start = ((), (), s32[]{:S(2)}) async-start(), calls=%async_computation.24 | async-start | bytes 2621440
  885.4 0.7 copy-start.19
  892.4 7.9 copy-start.12
  900.2 4.6 copy-start.29
  900.3 280.0 %all-reduce.9.cloned.1.call-start = ((), (), s32[]{:S(2)}) async-start(), calls=%async_computation.25 | async-start | bytes 16777216 | tf_op jit(solution)/shard_map/psum | solution.py:403
  900.3 4.5 copy-start.28
  910.5 366.4 %all-reduce.7.cloned.1.call-start = ((), (), s32[]{:S(2)}) async-start(), calls=%async_computation.17 | async-start | bytes 262144 | tf_op jit(solution)/shard_map/psum | solution.py:407
  927.2 243.4 %copy-start.17 = (f32[2048]{0:T(1024)S(1)}, f32[2048]{0:T(1024)}, u32[]{:S(2)}) copy-start(f32[2048]{0:T(1024)} %param.13) | copy-start | bytes 24580
  927.2 243.4 %copy-start.23 = (f32[128]{0:T(128)S(1)}, f32[128]{0:T(128)}, u32[]{:S(2)}) copy-start(f32[128]{0:T(128)} %copy-done.22) | copy-start | bytes 1540
  927.2 245.2 %copy-start.27 = (f32[128]{0:T(128)S(1)}, f32[128]{0:T(128)}, u32[]{:S(2)}) copy-start(f32[128]{0:T(128)} %copy-done.26) | copy-start | bytes 1540
  927.2 245.2 %copy-start.5 = (f32[1,128,2048]{1,2,0:T(8,128)S(1)}, f32[1,128,2048]{1,2,0:T(8,128)}, u32[]{:S(2)}) copy-start(f32[1,128,2048]{1,2,0:T(8,128)} %copy.83) | copy-start | bytes 3145732
  927.2 245.2 %copy-start.7 = (f32[128,2048]{0,1:T(8,128)S(1)}, f32[128,2048]{0,1:T(8,128)}, u32[]{:S(2)}) copy-start(f32[128,2048]{0,1:T(8,128)} %copy-done.6) | copy-start | bytes 3145732
  1184.4 94.1 %copy-start.1 = (bf16[512,2048]{1,0:T(8,128)(2,1)S(1)}, bf16[512,2048]{1,0:T(8,128)(2,1)}, u32[]{:S(2)}) copy-start(bf16[512,2048]{1,0:T(8,128)(2,1)} %param.16) | copy-start | bytes 6291460
Sparse Core Ops, SparseCore 0:
  12.9 48.9 all-gather.6
  66.4 33.3 all-gather.10
  102.2 35.1 all-gather.8
  155.9 43.6 reduce-scatter.27
  749.1 45.9 all-gather.16
  820.8 33.3 reduce-scatter.17
  857.2 35.1 reduce-scatter.19
  894.7 12.0 reduce-scatter.25
  909.6 13.4 reduce-scatter.21
  925.3 13.1 reduce-scatter.23
  941.4 181.5 reduce-scatter.29
  1125.1 43.4 reduce-scatter.33
Sparse Core Ops, SparseCore 1:
  160.6 156.1 all-gather.14
  319.9 146.5 all-gather.12
  552.2 188.9 reduce-scatter.31
  910.6 183.5 all-reduce.8
  1127.0 149.9 all-reduce.6

commit v2 on v1

--- a/solution.py
+++ b/solution.py
@@ -234,6 +234,489 @@
     return upper, lower
 
 
+MESH_ID = pl.DeviceIdType.MESH
+GROUP = 4
+VMEM_BYTES = 64 * 1024 * 1024 - 256 * 1024
+
+
+class Place:
+    def __init__(self):
+        self.ctx = lax.axis_index("context")
+        self.lev = lax.axis_index("expert")
+        self.side = self.ctx + 1 - 2 * (self.ctx % 2)
+        self.front = (self.ctx + 2) % GROUP
+        self.has_above = self.lev < GROUP - 1
+        self.has_below = self.lev > 0
+
+    def side_id(self):
+        return {"context": self.side}
+
+    def front_id(self):
+        return {"context": self.front}
+
+    def above_id(self):
+        return {"expert": jnp.minimum(self.lev + 1, GROUP - 1)}
+
+    def below_id(self):
+        return {"expert": jnp.maximum(self.lev - 1, 0)}
+
+    def nearest(self, rank):
+        flipped = self.lev >= 2
+        near = jnp.where(flipped, GROUP - 1 - self.lev, self.lev)
+        level = jnp.where(near == 0, rank, jnp.where(rank < 2, 1 - rank, rank))
+        return jnp.where(flipped, GROUP - 1 - level, level)
+
+    def greet(self, plane=True, line=True):
+        barrier = pltpu.get_barrier_semaphore()
+
+        def call(target):
+            pl.semaphore_signal(barrier, inc=1, device_id=target, device_id_type=MESH_ID)
+
+        if plane:
+            call(self.side_id())
+            call(self.front_id())
+        if line:
+            pl.when(self.has_above)(lambda: call(self.above_id()))
+            pl.when(self.has_below)(lambda: call(self.below_id()))
+        peers = 2 if plane else 0
+        if line:
+            peers = peers + 1 + jnp.where((self.lev > 0) & (self.lev < GROUP - 1), 1, 0)
+        pl.semaphore_wait(barrier, peers)
+
+
+def remote(src, dst, send_sem, recv_sem, target):
+    return pltpu.make_async_remote_copy(
+        src_ref=src,
+        dst_ref=dst,
+        send_sem=send_sem,
+        recv_sem=recv_sem,
+        device_id=target,
+        device_id_type=MESH_ID,
+    )
+
+
+def slot(level, member, tok, start=0, count=None):
+    count = tok if count is None else count
+    return pl.ds(pl.multiple_of(level * GROUP * tok + member * tok + start, tok // 2), count)
+
+
+def experts_kernel(
+    tok, width, experts,
+    x_ref, g_ref, wg_ref, wu_ref, wd_ref,
+    xo_ref, go_ref, ho_ref, dgo_ref, duo_ref, dw_ref,
+    x_all, g_all, wg, wu, wd, hid, dgate, dup,
+    line_send, line_recv, side_send, side_recv, front_send, front_recv,
+    part_send, part_recv, w_sem, g_sem, out_sem,
+):
+    at = Place()
+    half = tok // 2
+    ff = wg.shape[1]
+    chunk = min(256, ff)
+    own_expert = at.ctx * GROUP + at.lev
+    loads = [
+        pltpu.make_async_copy(src, dst, w_sem.at[i])
+        for i, (src, dst) in enumerate(((wg_ref, wg), (wu_ref, wu), (wd_ref, wd)))
+    ]
+
+    def g_load(level, member):
+        column = (
+            at.ctx if member == 0 else at.side if member == 1 else at.front if member == 2
+            else GROUP - 1 - at.ctx
+        )
+        start = pl.multiple_of((column * GROUP + level) * tok, tok)
+        return pltpu.make_async_copy(
+            g_ref.at[pl.ds(start, tok)],
+            g_all.at[slot(level, member, tok)],
+            g_sem.at[level, member],
+        )
+
+    def line_copy(rank, level, up):
+        place = x_all.at[slot(level, 0, tok)]
+        return remote(
+            place, place, line_send.at[0 if up else 1, rank], line_recv.at[level],
+            at.above_id() if up else at.below_id(),
+        )
+
+    def plane_copy(level, member):
+        sems = (side_send, side_recv) if member == 1 else (front_send, front_recv)
+        return remote(
+            x_all.at[slot(level, 0, tok)], x_all.at[slot(level, member, tok)],
+            sems[0].at[level], sems[1].at[level],
+            at.side_id() if member == 1 else at.front_id(),
+        )
+
+    def part_copy(level, member):
+        start = 0 if member == 1 else half
+        return remote(
+            x_all.at[slot(level, member, tok, start, half)],
+            x_all.at[slot(level, 3, tok, start, half)],
+            part_send.at[member - 1, level], part_recv.at[member - 1, level],
+            at.front_id() if member == 1 else at.side_id(),
+        )
+
+    def pass_on(rank, act):
+        level = at.nearest(rank)
+
+        @pl.when((level <= at.lev) & at.has_above)
+        def _():
+            act(line_copy(rank, level, True))
+
+        @pl.when((level >= at.lev) & at.has_below)
+        def _():
+            act(line_copy(rank, level, False))
+
+        act(plane_copy(level, 1))
+        act(plane_copy(level, 2))
+
+    begin = lambda copy: copy.start()
+    x_own = pltpu.make_async_copy(x_ref, x_all.at[slot(at.lev, 0, tok)], w_sem.at[3])
+    x_own.start()
+    at.greet()
+    x_own.wait()
+    pass_on(0, begin)
+    for load in loads:
+        load.start()
+
+    def all_g(rank, carry):
+        level = at.nearest(rank)
+        for member in range(GROUP):
+            g_load(level, member).start()
+        return carry
+
+    lax.fori_loop(0, GROUP, all_g, 0)
+    second = at.nearest(1)
+    line_copy(1, second, True).wait_recv()
+    pass_on(1, begin)
+    for load in loads:
+        load.wait()
+
+    def out_copies(rows, step):
+        pairs = (
+            (x_all.at[rows, pl.ds(0, width)], xo_ref.at[rows]),
+            (g_all.at[rows], go_ref.at[rows]),
+            (hid.at[rows], ho_ref.at[rows]),
+            (dgate.at[rows], dgo_ref.at[rows]),
+            (dup.at[rows], duo_ref.at[rows]),
+        )
+        return [
+            pltpu.make_async_copy(src, dst, out_sem.at[i, step])
+            for i, (src, dst) in enumerate(pairs)
+        ]
+
+    lane = lax.broadcasted_iota(jnp.int32, (2 * tok, 128), 1)
+
+    def compute(level, late):
+        for member in range(2):
+            pl.when(late == 0)(lambda m=member: g_load(level, m).wait())
+            pl.when(late == 1)(lambda m=member: g_load(level, m + 2).wait())
+        rows = pl.ds(pl.multiple_of(level * GROUP * tok + late * 2 * tok, 2 * tok), 2 * tok)
+        tail = x_all[rows, pl.ds(width, 128)].astype(jnp.float32)
+        own = (lane == own_expert) | (lane == own_expert + experts)
+        factor = jnp.sum(jnp.where(own, tail, 0.0), axis=1, keepdims=True)
+
+        def column(index, total):
+            cols = pl.ds(pl.multiple_of(index * chunk, chunk), chunk)
+            feats = x_all[rows, pl.ds(0, width)]
+            gate_pre = nn_dot(feats, wg[:, cols])
+            up_pre = nn_dot(feats, wu[:, cols])
+            back = nt_dot(g_all[rows, :], wd[cols, :])
+            sig = 1.0 / (1.0 + jnp.exp(-gate_pre))
+            active = gate_pre * sig
+            hidden = active * up_pre
+            hid[rows, cols] = (factor * hidden).astype(jnp.bfloat16)
+            grad = factor * back
+            dgate[rows, cols] = (
+                grad * up_pre * sig * (1.0 + gate_pre * (1.0 - sig))
+            ).astype(jnp.bfloat16)
+            dup[rows, cols] = (grad * active).astype(jnp.bfloat16)
+            return total + jnp.sum(hidden * back, axis=1, keepdims=True)
+
+        d_weight = lax.fori_loop(
+            0, ff // chunk, column, jnp.zeros((2 * tok, 1), jnp.float32)
+        )
+        upper = d_weight.astype(jnp.bfloat16).astype(jnp.float32)
+        lower = d_weight - upper
+        dw_ref[rows, :] = jnp.where(
+            lane == own_expert, upper, jnp.where(lane == own_expert + experts, lower, 0.0)
+        ).astype(jnp.bfloat16)
+        for copy in out_copies(rows, level * 2 + late):
+            copy.start()
+
+    def step(index, carry):
+        rank = index // 2
+        late = index % 2
+
+        @pl.when((late == 0) & (rank < GROUP))
+        def _():
+            level = at.nearest(rank)
+            plane_copy(level, 1).wait_recv()
+            part_copy(level, 1).start()
+            plane_copy(level, 2).wait_recv()
+            part_copy(level, 2).start()
+
+            @pl.when(rank < GROUP - 2)
+            def _():
+                coming = at.nearest(rank + 2)
+                line_copy(rank + 2, coming, True).wait_recv()
+                pass_on(rank + 2, begin)
+
+        @pl.when((late == 1) & (rank >= 1))
+        def _():
+            level = at.nearest(rank - 1)
+            part_copy(level, 1).wait_recv()
+            part_copy(level, 2).wait_recv()
+
+        @pl.when(((late == 0) & (rank < GROUP)) | ((late == 1) & (rank >= 1)))
+        def _():
+            compute(at.nearest(rank - late), late)
+
+        return carry
+
+    lax.fori_loop(0, 2 * GROUP + 2, step, 0)
+
+    def drain(rank, carry):
+        pass_on(rank, lambda copy: copy.wait_send())
+        level = at.nearest(rank)
+        part_copy(level, 1).wait_send()
+        part_copy(level, 2).wait_send()
+        for late in range(2):
+            rows = pl.ds(pl.multiple_of(level * GROUP * tok + late * 2 * tok, 2 * tok), 2 * tok)
+            for copy in out_copies(rows, level * 2 + late):
+                copy.wait()
+        return carry
+
+    lax.fori_loop(0, GROUP, drain, 0)
+
+
+def run_experts(sending, all_upstream, w_gate, w_up, w_down):
+    tok, wide = sending.shape
+    width = all_upstream.shape[1]
+    ff = w_gate.shape[1]
+    total = GROUP * GROUP * tok
+    anywhere = pl.BlockSpec(memory_space=pl.ANY)
+    bf16 = jnp.bfloat16
+    dma = pltpu.SemaphoreType.DMA
+    sent = (GROUP * 2 + 1) * tok * wide * 2
+    return pl.pallas_call(
+        functools.partial(experts_kernel, tok, width, GROUP * GROUP),
+        in_specs=[anywhere] * 5,
+        out_specs=[anywhere] * 5 + [pl.BlockSpec(memory_space=pltpu.VMEM)],
+        out_shape=[
+            jax.ShapeDtypeStruct((total, width), bf16),
+            jax.ShapeDtypeStruct((total, width), bf16),
+            jax.ShapeDtypeStruct((total, ff), bf16),
+            jax.ShapeDtypeStruct((total, ff), bf16),
+            jax.ShapeDtypeStruct((total, ff), bf16),
+            jax.ShapeDtypeStruct((total, 128), bf16),
+        ],
+        scratch_shapes=[
+            pltpu.VMEM((total, wide), bf16),
+            pltpu.VMEM((total, width), bf16),
+            pltpu.VMEM((width, ff), bf16),
+            pltpu.VMEM((width, ff), bf16),
+            pltpu.VMEM((ff, width), bf16),
+            pltpu.VMEM((total, ff), bf16),
+            pltpu.VMEM((total, ff), bf16),
+            pltpu.VMEM((total, ff), bf16),
+            dma((2, GROUP)),
+            dma((GROUP,)),
+            dma((GROUP,)),
+            dma((GROUP,)),
+            dma((GROUP,)),
+            dma((GROUP,)),
+            dma((2, GROUP)),
+            dma((2, GROUP)),
+            dma((4,)),
+            dma((GROUP, GROUP)),
+            dma((5, 2 * GROUP)),
+        ],
+        compiler_params=pltpu.CompilerParams(
+            collective_id=1, has_side_effects=True, vmem_limit_bytes=VMEM_BYTES
+        ),
+        cost_estimate=pl.CostEstimate(
+            flops=6 * total * width * ff, bytes_accessed=60 << 20, transcendentals=0
+        ),
+        name="experts",
+    )(sending, all_upstream, w_gate, w_up, w_down)
+
+
+def give_back_kernel(tok, width, terms, tailed, *refs):
+    refs = list(refs)
+    take = lambda n: [refs.pop(0) for _ in range(n)]
+    lhs_in, w_in = take(terms), take(terms)
+    tail_ref = take(1)[0] if tailed else None
+    out_ref = take(1)[0]
+    lhs, weight = take(terms), take(terms)
+    (
+        mine, part_a, part_b, from_side, from_front, from_above, from_below,
+        load_sem, part_send, part_recv, plane_send, plane_recv, line_send, line_recv,
+    ) = refs
+    at = Place()
+    half = tok // 2
+    wide = mine.shape[1]
+    chunk = 256
+    f32 = lambda value: value.astype(jnp.float32)
+    loads = [
+        pltpu.make_async_copy(src, dst, load_sem.at[i])
+        for i, (src, dst) in enumerate(zip(lhs_in + w_in, lhs + weight))
+    ]
+    for load in loads:
+        load.start()
+    at.greet()
+    for load in loads:
+        load.wait()
+
+    def compute(level, late):
+        rows = pl.ds(pl.multiple_of(level * GROUP * tok + late * 2 * tok, 2 * tok), 2 * tok)
+        if tailed:
+            mine[rows, pl.ds(width, 128)] = tail_ref[rows, :]
+
+        def column(index, carry):
+            cols = pl.ds(pl.multiple_of(index * chunk, chunk), chunk)
+            if terms == 2:
+                result = nt_dot(lhs[0][rows, :], weight[0][cols, :]) + nt_dot(
+                    lhs[1][rows, :], weight[1][cols, :]
+                )
+            else:
+                result = nn_dot(lhs[0][rows, :], weight[0][:, cols])
+            mine[rows, cols] = result.astype(jnp.bfloat16)
+            return carry
+
+        lax.fori_loop(0, width // chunk, column, 0)
+
+    def part_copy(level, member):
+        start = 0 if member == 2 else half
+        target = part_a if member == 2 else part_b
+        return remote(
+            mine.at[slot(level, 3, tok, start, half)], target.at[level],
+            part_send.at[member - 1, level], part_recv.at[member - 1, level],
+            at.side_id() if member == 1 else at.front_id(),
+        )
+
+    def plane_copy(level, member):
+        target = from_side if member == 1 else from_front
+        return remote(
+            mine.at[slot(level, member, tok)], target.at[level],
+            plane_send.at[member - 1, level], plane_recv.at[member - 1, level],
+            at.side_id() if member == 1 else at.front_id(),
+        )
+
+    def line_copy(level, up):
+        target = from_below if up else from_above
+        return remote(
+            mine.at[slot(level, 0, tok)], target.at[level],
+            line_send.at[0 if up else 1, level], line_recv.at[0 if up else 1, level],
+            at.above_id() if up else at.below_id(),
+        )
+
+    def add_into(place, other):
+        mine[place, :] = (f32(mine[place, :]) + f32(other)).astype(jnp.bfloat16)
+
+    def finish(level):
+        place = slot(level, 0, tok)
+        plane_copy(level, 1).wait_recv()
+        plane_copy(level, 2).wait_recv()
+        out_ref[...] = f32(mine[place, :]) + f32(from_side[level]) + f32(from_front[level])
+
+        @pl.when((level <= at.lev) & at.has_above)
+        def _():
+            line_copy(level, False).wait_recv()
+            out_ref[...] += f32(from_above[level])
+
+        @pl.when((level >= at.lev) & at.has_below)
+        def _():
+            line_copy(level, True).wait_recv()
+            out_ref[...] += f32(from_below[level])
+
+        @pl.when(level != at.lev)
+        def _():
+            mine[place, :] = out_ref[...].astype(jnp.bfloat16)
+
+        pl.when(level < at.lev)(lambda: line_copy(level, False).start())
+        pl.when(level > at.lev)(lambda: line_copy(level, True).start())
+
+    def step(rank, carry):
+        @pl.when(rank < GROUP)
+        def _():
+            level = at.nearest(GROUP - 1 - rank)
+            compute(level, 1)
+            part_copy(level, 2).start()
+            part_copy(level, 1).start()
+
+        @pl.when(rank >= 1)
+        def _():
+            finish(at.nearest(GROUP - rank))
+
+        @pl.when(rank < GROUP)
+        def _():
+            level = at.nearest(GROUP - 1 - rank)
+            compute(level, 0)
+            part_copy(level, 2).wait_recv()
+            add_into(slot(level, 1, tok, 0, half), part_a[level])
+            plane_copy(level, 1).start()
+            part_copy(level, 1).wait_recv()
+            add_into(slot(level, 2, tok, half, half), part_b[level])
+            plane_copy(level, 2).start()
+
+        return carry
+
+    lax.fori_loop(0, GROUP + 1, step, 0)
+
+    def drain(level, carry):
+        for member in (1, 2):
+            part_copy(level, member).wait_send()
+            plane_copy(level, member).wait_send()
+        pl.when(level < at.lev)(lambda: line_copy(level, False).wait_send())
+        pl.when(level > at.lev)(lambda: line_copy(level, True).wait_send())
+        return carry
+
+    lax.fori_loop(0, GROUP, drain, 0)
+
+
+def give_back(lhs, weights, tail, ident, name):
+    total, ff = lhs[0].shape
+    terms = len(lhs)
+    width = weights[0].shape[0] if terms == 2 else weights[0].shape[1]
+    tok = total // (GROUP * GROUP)
+    wide = width + (0 if tail is None else 128)
+    bf16 = jnp.bfloat16
+    dma = pltpu.SemaphoreType.DMA
+    anywhere = pl.BlockSpec(memory_space=pl.ANY)
+    vmem = pl.BlockSpec(memory_space=pltpu.VMEM)
+    tails = () if tail is None else (tail,)
+    return pl.pallas_call(
+        functools.partial(give_back_kernel, tok, width, terms, tail is not None),
+        in_specs=[anywhere] * (2 * terms) + [vmem] * len(tails),
+        out_specs=vmem,
+        out_shape=jax.ShapeDtypeStruct((tok, wide), jnp.float32),
+        scratch_shapes=[pltpu.VMEM((total, ff), bf16)] * terms
+        + [pltpu.VMEM(w.shape, bf16) for w in weights]
+        + [
+            pltpu.VMEM((total, wide), bf16),
+            pltpu.VMEM((GROUP, tok // 2, wide), bf16),
+            pltpu.VMEM((GROUP, tok // 2, wide), bf16),
+            pltpu.VMEM((GROUP, tok, wide), bf16),
+            pltpu.VMEM((GROUP, tok, wide), bf16),
+            pltpu.VMEM((GROUP, tok, wide), bf16),
+            pltpu.VMEM((GROUP, tok, wide), bf16),
+            dma((2 * terms,)),
+            dma((2, GROUP)),
+            dma((2, GROUP)),
+            dma((2, GROUP)),
+            dma((2, GROUP)),
+            dma((2, GROUP)),
+            dma((2, GROUP)),
+        ],
+        compiler_params=pltpu.CompilerParams(
+            collective_id=ident, has_side_effects=True, vmem_limit_bytes=VMEM_BYTES
+        ),
+        cost_estimate=pl.CostEstimate(
+            flops=2 * terms * total * width * ff, bytes_accessed=20 << 20, transcendentals=0
+        ),
+        name=name,
+    )(*lhs, *weights, *tails)
+
+
 TOKEN_AXES = ("context", "expert")
 
 
@@ -259,7 +742,6 @@
     expert_count = router.shape[1]
     span_rows = tok_count * expert_size
     context_index = lax.axis_index("context")
-    own_expert = context_index * expert_size + lax.axis_index("expert")
     place = jnp.full((1,), context_index, jnp.int32)
     local_places = folded_positions(
         context_index * span_rows + jnp.arange(span_rows, dtype=jnp.int32), span_rows, context_size
@@ -300,42 +782,11 @@
     expert_in = mixed_in.astype(jnp.bfloat16)
     pad = jnp.zeros((tok_count, 128 - 2 * expert_count), jnp.bfloat16)
     sending = jnp.concatenate([expert_in, *split_pair(weights), pad], axis=1)
-    arrived = lax.all_gather(sending, TOKEN_AXES, axis=0, tiled=True)
-    rows = arrived[:, :model_width]
-    pairs = arrived[:, model_width:].astype(jnp.float32)
-    lane = jnp.arange(128, dtype=jnp.int32)[None, :]
-    mine = (lane == own_expert) | (lane == own_expert + expert_count)
-    factor = jnp.sum(jnp.where(mine, pairs, 0.0), axis=1, keepdims=True)
-    gate_pre = nn_dot(rows, w_gate[0])
-    up_pre = nn_dot(rows, w_up[0])
-    back_hidden = nt_dot(all_upstream, w_down[0])
-    sigmoid_g = jax.nn.sigmoid(gate_pre)
-    activated = gate_pre * sigmoid_g
-    hidden = activated * up_pre
-    d_weight = jnp.sum(hidden * back_hidden, axis=1, keepdims=True)
-    hidden_w = (factor * hidden).astype(jnp.bfloat16)
-    grad_hidden = factor * back_hidden
-    grad_gate = (grad_hidden * up_pre * sigmoid_g * (1.0 + gate_pre * (1.0 - sigmoid_g))).astype(
-        jnp.bfloat16
-    )
-    grad_up = (grad_hidden * activated).astype(jnp.bfloat16)
-    grad_rows = (nt_dot(grad_gate, w_gate[0]) + nt_dot(grad_up, w_up[0])).astype(jnp.bfloat16)
-    upper, lower = split_pair(d_weight)
-    d_pairs = jnp.where(lane == own_expert, upper, jnp.zeros((), jnp.bfloat16)) + jnp.where(
-        lane == own_expert + expert_count, lower, jnp.zeros((), jnp.bfloat16)
-    )
-    returned = lax.psum_scatter(
-        jnp.concatenate([grad_rows, d_pairs], axis=1),
-        TOKEN_AXES,
-        scatter_dimension=0,
-        tiled=True,
-    ).astype(jnp.float32)
-    hidden_out = resid + lax.psum_scatter(
-        nn_dot(hidden_w, w_down[0]).astype(jnp.bfloat16),
-        TOKEN_AXES,
-        scatter_dimension=0,
-        tiled=True,
-    ).astype(jnp.float32)
+    rows, upstream_rows, hidden_w, grad_gate, grad_up, d_pairs = run_experts(
+        sending, all_upstream, w_gate[0], w_up[0], w_down[0]
+    )
+    returned = give_back((grad_gate, grad_up), (w_gate[0], w_up[0]), d_pairs, 2, "give_back")
+    hidden_out = resid + give_back((hidden_w,), (w_down[0],), None, 3, "combine")
 
     def over_sequences(grad):
         return lax.psum_scatter(
@@ -344,7 +795,7 @@
 
     gate_sum = over_sequences(tn_dot(rows, grad_gate))
     up_sum = over_sequences(tn_dot(rows, grad_up))
-    down_sum = over_sequences(tn_dot(hidden_w, all_upstream))
+    down_sum = over_sequences(tn_dot(hidden_w, upstream_rows))
 
     d_weights = (
         returned[:, model_width : model_width + expert_count]

time: 1300 us -> 966 us (0.74)
  waiting for transfers between devices: 907 us -> 390 us
  Pallas kernels: 36.7 us -> 338 us
  matrix products: 179 us -> 83.4 us
  local copies, waits for them, and re-layouts: 51.7 us -> 26 us
  blocking collectives: 52.5 us -> 68.1 us
    unnamed x21 -> x14, waiting for transfers between devices: 437 us -> 0.91 us
    pallas_call x0 -> x3, Pallas kernels: none -> 301 us  [the longest x2 218 us: give_back(): pl.pallas_call(functools.partial(give_back_kernel, tok, width, terms, tai...]
    all_gather x1 -> x0, waiting for transfers between devices: 135 us -> none  [fast_device(): arrived = lax.all_gather(sending, TOKEN_AXES, axis=0, tiled=True)]
    dot_general x5 -> x2, matrix products: 60.6 us -> 8.03 us  [nn_dot(): return jnp.dot(left, right, preferred_element_type=jnp.float32)]
    reduce_scatter x0 -> x2, waiting for transfers between devices: none -> 49.1 us  [the longest x1 49.1 us: fast_device(): lax.psum_scatter(nn_dot(attended, w_out).astype(jnp.bfloat16), 'expert',...]
    dot_general x4 -> x1, matrix products: 47.9 us -> 3.67 us  [nt_dot(): lax.dot_general(left, right, (((1,), (1,)), ((), ())), preferred_element_...]
    all_gather x1, waiting for transfers between devices: 113 us -> 84 us  [fast_device(): lax.all_gather(upstream.astype(jnp.bfloat16), TOKEN_AXES, axis=0, tiled=T...]
    psum x1, waiting for transfers between devices: 43.3 us -> 67.9 us  [fast_device(): lax.psum((attn_gain_part, moe_gain_part, router_part), ('dp', 'context',...]
  transfers between devices with their start and end apart: 17 -> 14, of which waited for: 14 -> 9; matrix products, arithmetic and copies ran while one was open for 13% -> 12% of each run, Pallas kernels for 0% -> 14%
where the time goes in v2:
time: 966 us; the launch traced here: 957 us
  waiting for transfers between devices  390 us (40%)
  Pallas kernels  338 us (35%)
  matrix products  83.4 us (9%)
  blocking collectives  68.1 us (7%)
  other arithmetic  33.8 us (3%)
  local copies, waits for them, and re-layouts  26 us (3%)
  between operations  16.7 us (2%)
    pallas_call x2, Pallas kernels, give_back(): pl.pallas_call(functools.partial(give_back_kernel, tok, width, terms, tai...  218 us
    all_gather x1, waiting for transfers between devices, fast_device(): lax.all_gather(upstream.astype(jnp.bfloat16), TOKEN_AXES, axis=0, tiled=T...  84 us
    pallas_call x1, Pallas kernels, run_experts(): pl.pallas_call(functools.partial(experts_kernel, tok, width, GROUP * GROU...  82.7 us
    psum x1, waiting for transfers between devices, fast_device(): lax.psum((attn_gain_part, moe_gain_part, router_part), ('dp', 'context',...  67.9 us
    psum x1, blocking collectives, fast_device(): lax.psum((attn_gain_part, moe_gain_part, router_part), ('dp', 'context',...  50.4 us
    reduce_scatter x1, waiting for transfers between devices, fast_device(): lax.psum_scatter(nn_dot(attended, w_out).astype(jnp.bfloat16), 'expert',...  49.1 us
    all_gather x1, waiting for transfers between devices, fast_device(): lax.all_gather(d_resid.astype(jnp.bfloat16), 'expert', axis=0, tiled=True)  48.7 us
    all_gather x1, waiting for transfers between devices, fast_device(): gathered_in = lax.all_gather(normed_b, 'expert', axis=0, tiled=True)  48.5 us
  transfers between devices with their start and end apart: 14, of which 9 were waited for; matrix products, arithmetic and copies ran while one was open for 12% of the time, Pallas kernels for 14%

profile of v2, /device:TPU:0, one launch (start us, length us, event | category | flops | bytes accessed | tf_op | source)
XLA Modules:
  0.0 957.0 jit_solution(6196302876011326522)
XLA Ops:
  8.1 1.3 fusion.18
  9.3 0.5 copy-done.48
  9.9 0.6 copy-done.40
  10.4 2.0 fusion.13
  12.5 48.5 %all-gather.6.cloned.1.call-done = bf16[512,2048]{1,0:T(8,128)(2,1)} async-done(((bf16[128,2048]{1,0:T(8,128)(2,1)}), bf16[512,2048]{1,0:T(8,128)(2,1)}) %all-gather.6.cloned.1.call-update) | async-done | bytes 2097168 | tf_op jit(solution)/shard_map/all_gather | solution.py:751
  61.0 4.4 fusion.8
  65.6 0.5 multiply_cosine_fusion
  66.2 4.7 multiply_reduce_fusion.2
  71.1 1.1 copy-done.2
  72.7 1.0 copy.65
  73.7 1.0 copy.64.q_ref
  74.8 24.8 %all-gather.10.cloned.1.call-done.v_ref = bf16[2048,512]{1,0:T(8,128)(2,1)} async-done(((bf16[512,512]{1,0:T(8,128)(2,1)}), bf16[2048,512]{1,0:T(8,128)(2,1)}) %all-gather.10.cloned.1.call-update) | async-done | bytes 2097168 | tf_op jit(solution)/shard_map/all_gather | solution.py:766
  99.6 37.6 %all-gather.8.cloned.1.call-done.k_ref = bf16[2048,512]{1,0:T(8,128)(2,1)} async-done(((bf16[512,512]{1,0:T(8,128)(2,1)}), bf16[2048,512]{1,0:T(8,128)(2,1)}) %all-gather.8.cloned.1.call-update) | async-done | bytes 2097168 | tf_op jit(solution)/shard_map/all_gather | solution.py:765
  137.2 14.9 %attend.1 = (bf16[512,512]{1,0:T(8,128)(2,1)}, f32[4,1,512]{2,1,0:T(1,128)}) custom-call(s32[1]{0:T(128)} %bitcast.1.place_ref, bf16[512,512]{1,0:T(8,128)(2,1)} %copy.64.q_ref, bf16[2048,512]{1,0:T(8,128)(2,1)} %all-gather.8.cloned.1.call-done.k_ref, bf16[2048,512]{1,0:T(8,128)(2,1)} %all-gather.10.cloned.1.call-done.v_ref), custom_call_target="tpu_custom_call" | custom-call | tf_op jit(solution)/shard_map/attend/pallas_call | solution.py:136
  152.1 3.6 convolution_convert_fusion.1
  155.8 1.1 copy-done.12
  157.0 0.9 bitcast_convert_fusion.1
  158.1 49.1 %reduce-scatter.8.cloned.1.call-done = bf16[128,2048]{1,0:T(8,128)(2,1)} async-done(((bf16[512,2048]{1,0:T(8,128)(2,1)}), bf16[128,2048]{1,0:T(8,128)(2,1)}) %reduce-scatter.8.cloned.1.call-update) | async-done | bytes 524304 | tf_op jit(solution)/shard_map/reduce_scatter | solution.py:768
  207.1 1.4 multiply_reduce_fusion.5
  208.5 0.5 copy-done.50
  209.0 2.1 fusion.48
  211.8 0.5 copy-done.38
  212.6 1.0 concatenate.13.x_ref
  213.6 84.0 %all-gather.12.cloned.1.call-done.g_ref = bf16[2048,2048]{1,0:T(8,128)(2,1)} async-done(((bf16[128,2048]{1,0:T(8,128)(2,1)}), bf16[2048,2048]{1,0:T(8,128)(2,1)}) %all-gather.12.cloned.1.call-update) | async-done | bytes 8388624 | tf_op jit(solution)/shard_map/all_gather | solution.py:752
  297.6 82.7 %experts.1 = (bf16[2048,2048]{1,0:T(8,128)(2,1)}, bf16[2048,2048]{1,0:T(8,128)(2,1)}, bf16[2048,1024]{1,0:T(8,128)(2,1)}, bf16[2048,1024]{1,0:T(8,128)(2,1)}, bf...) custom-call(bf16[128,2176]{1,0:T(8,128)(2,1)} %concatenate.13.x_ref, ...), custom_call_target="tpu_custom_call" | custom-call | flops 25769803776 | bytes 62914560 | tf_op jit(solution)/shard_map/experts/pallas_call | solution.py:500
  380.4 86.5 %give_back.1 = f32[128,2176]{1,0:T(8,128)} custom-call(bf16[2048,1024]{1,0:T(8,128)(2,1)} %get-tuple-element.24.refs_0_, bf16[2048,1024]{1,0:T(8,128)(2,1)} %get-tuple-element.25.refs_1_, bf16[2048,1024]{1,0:T(8,128)(2,1)} %bitcast.110, bf16[2048,1024]{1,0:T(8,128)(2,1)} %bitcast.112, bf16[2048,128]{1,0:T(8,128)(2,1)} %get-tuple-element.26.refs_4_), custom_call_target="tpu_custom_call" | custom-call | flops 17179869184 | bytes 20971520 | tf_op jit(solution)/shard_map/give_back/pallas_call | solution.py:687
  467.0 1.2 multiply_reduce_fusion.6
  468.2 3.6 multiply_reduce_fusion.3
  471.8 0.9 copy-done.10
  472.8 1.2 fusion.47
  474.1 48.7 %all-gather.14.cloned.1.call-done = bf16[512,2048]{1,0:T(8,128)(2,1)} async-done(((bf16[128,2048]{1,0:T(8,128)(2,1)}), bf16[512,2048]{1,0:T(8,128)(2,1)}) %all-gather.14.cloned.1.call-update) | async-done | bytes 2097168 | tf_op jit(solution)/shard_map/all_gather | solution.py:823
  522.8 3.7 convolution_convert_fusion.2.g_ref
  526.5 21.9 %attend_back.1 = (f32[512,512]{1,0:T(8,128)}, bf16[2048,512]{1,0:T(8,128)(2,1)}, bf16[2048,512]{1,0:T(8,128)(2,1)}) custom-call(s32[1]{0:T(128)} %bitcast.1.place_ref, bf16[512,512]{1,0:T(8,128)(2,1)} %copy.64.q_ref, bf16[512,512]{1,0:T(8,128)(2,1)} %convolution_convert_fusion.2.g_ref, bf16[512,512]{1,0:T(8,128)(2,1)} %get-tuple-element.22.o_ref, ...), custom_call_target="tpu_custom_call" | custom-call | tf_op jit(solution)/shard_map/attend_back/pallas_call | solution.py:208
  548.5 0.7 reduce-scatter.12.cloned.1.call-update
  549.2 14.0 %convert_bitcast_fusion.1 = bf16[1,1024,2048]{2,1,0:T(8,128)(2,1)} fusion(bf16[2048,1024]{1,0:T(8,128)(2,1)} %get-tuple-element.23.refs_0_, bf16[2048,2048]{1,0:T(8,128)(2,1)} %get-tuple-element.32), kind=kOutput, calls=%fused_computation.2 | convolution fusion | flops 8592031744 | bytes 16777216 | tf_op jit(solution)/shard_map/dot_general | solution.py:75
  563.5 14.1 %convert_bitcast_fusion.2 = bf16[1,2048,1024]{2,1,0:T(8,128)(2,1)} fusion(bf16[2048,2048]{1,0:T(8,128)(2,1)} %get-tuple-element.31, bf16[2048,1024]{1,0:T(8,128)(2,1)} %get-tuple-element.25.refs_1_), kind=kOutput, calls=%fused_computation.3 | convolution fusion | flops 8592031744 | bytes 16777216 | tf_op jit(solution)/shard_map/dot_general | solution.py:75
  577.7 14.1 %convert_bitcast_fusion.3 = bf16[1,2048,1024]{2,1,0:T(8,128)(2,1)} fusion(bf16[2048,2048]{1,0:T(8,128)(2,1)} %get-tuple-element.31, bf16[2048,1024]{1,0:T(8,128)(2,1)} %get-tuple-element.24.refs_0_), kind=kOutput, calls=%fused_computation.4 | convolution fusion | flops 8592031744 | bytes 16777216 | tf_op jit(solution)/shard_map/dot_general | solution.py:75
  592.1 1.2 copy-done.19
  593.6 1.3 copy.67
  595.0 0.5 multiply_add_fusion.1
  595.4 1.1 copy-done.3
  596.5 0.6 multiply_reduce_fusion
  597.7 0.5 copy.68
  598.3 23.0 %reduce-scatter.12.cloned.1.call-done = bf16[512,512]{1,0:T(8,128)(2,1)} async-done(((bf16[2048,512]{1,0:T(8,128)(2,1)}), bf16[512,512]{1,0:T(8,128)(2,1)}) %reduce-scatter.12.cloned.1.call-update) | async-done | bytes 524304 | tf_op jit(solution)/shard_map/reduce_scatter | solution.py:834
  621.3 7.7 bitcast_convert_fusion
  629.1 1.0 copy-done.20
  630.1 4.4 convolution_convert_fusion
  634.6 5.4 convert_bitcast_fusion
  640.1 0.6 copy-done.26
  640.7 1.6 fusion.21
  642.2 131.9 %combine.1 = f32[128,2048]{1,0:T(8,128)} custom-call(bf16[2048,1024]{1,0:T(8,128)(2,1)} %get-tuple-element.23.refs_0_, bf16[1024,2048]{1,0:T(8,128)(2,1)} %bitcast.114), custom_call_target="tpu_custom_call" | custom-call | flops 8589934592 | bytes 20971520 | tf_op jit(solution)/shard_map/combine/pallas_call | solution.py:687
  774.1 17.7 %psum.44 = bf16[2,512]{1,0:T(2,128)(2,1)S(1)} all-reduce(bf16[2,512]{1,0:T(2,128)(2,1)S(1)} %bitcast.107), channel_id=1, replica_groups=mesh['dp'=2,'context'=4,'expert'=4] {'dp','context'}, use_global_device_ids=true, to_apply=%region_18.19 | all-reduce | flops 1024 | bytes 4096 | tf_op jit(solution)/shard_map/psum | solution.py:856
  791.8 0.6 convert_element_type.121
  792.4 4.2 convert_element_type.129
  796.6 4.3 convert_element_type.127
  801.0 4.3 convert_element_type.125
  805.3 1.7 fusion.14
  807.0 3.4 fusion.17
  810.4 5.3 all-reduce.9.cloned.1.call-done
  815.7 4.1 convert_element_type.123
  819.8 9.5 copy.62
  829.3 50.4 %all-reduce.2 = (f32[2048]{0:T(1024)}, f32[2048]{0:T(1024)}) all-reduce(f32[2048]{0:T(1024)S(1)} %get-tuple-element.81, f32[2048]{0:T(1024)S(1)} %copy-done.32), channel_id=1, replica_groups=mesh['dp'=2,'context'=4,'expert'=4] {'dp','context','expert'}, use_global_device_ids=true, to_apply=%region_15.16 | all-reduce | flops 4096 | bytes 32768 | tf_op jit(solution)/shard_map/psum | solution.py:858
  879.7 67.9 %all-reduce.7.cloned.1.call-done = f32[2048,16]{0,1:T(8,128)} async-done(((f32[2048,16]{0,1:T(8,128)}), f32[2048,16]{0,1:T(8,128)}) %all-reduce.7.cloned.1.call-update) | async-done | bytes 131088 | tf_op jit(solution)/shard_map/psum | solution.py:858
  947.6 1.6 copy.76
  (157 shorter events, 4.2 us)
Async XLA Ops:
  8.0 201.0 %copy-start = (f32[2048,16]{0,1:T(8,128)S(1)}, f32[2048,16]{0,1:T(8,128)}, u32[]{:S(2)}) copy-start(f32[2048,16]{0,1:T(8,128)} %param.18) | copy-start | bytes 393220
  8.0 53.0 %all-gather.6.cloned.1.call-start = ((), (), s32[]{:S(2)}) async-start(), calls=%async_computation.7 | async-start | bytes 2621440 | tf_op jit(solution)/shard_map/all_gather | solution.py:751
  12.5 53.0 %copy-start.43 = (f32[2,512]{1,0:T(2,128)S(1)}, f32[2,512]{1,0:T(2,128)}, u32[]{:S(2)}) copy-start(f32[2,512]{1,0:T(2,128)} %param.15) | copy-start | bytes 12292
  12.5 87.1 %all-gather.10.cloned.1.call-start = ((), (), s32[]{:S(2)}) async-start(), calls=%async_computation.9 | async-start | bytes 2621440 | tf_op jit(solution)/shard_map/all_gather | solution.py:766
  61.0 5.1 copy-start.54
  65.5 71.8 %all-gather.8.cloned.1.call-start = ((), (), s32[]{:S(2)}) async-start(), calls=%async_computation.8 | async-start | bytes 2621440 | tf_op jit(solution)/shard_map/all_gather | solution.py:765
  65.5 5.4 copy-start.30
  66.1 6.1 copy-start.15
  66.1 6.1 copy-start.17
  70.8 1.4 copy-start.2
  70.8 1.4 copy-start.28
  70.9 1.3 copy-start.21
  73.7 133.4 %reduce-scatter.8.cloned.1.call-start = ((), (), s32[]{:S(2)}) async-start(), calls=%async_computation.10 | async-start | bytes 2621440 | tf_op jit(solution)/shard_map/reduce_scatter | solution.py:768
  137.2 14.9 %copy-start.52 = (bf16[512,2048]{1,0:T(8,128)(2,1)S(1)}, bf16[512,2048]{1,0:T(8,128)(2,1)}, u32[]{:S(2)}) copy-start(bf16[512,2048]{1,0:T(8,128)(2,1)} %param.16) | copy-start | bytes 6291460
  155.8 1.2 copy-start.12
  155.8 2.2 copy-start.42
  155.8 51.4 %copy-start.4 = (bf16[1,128,2048]{2,1,0:T(8,128)(2,1)S(1)}, bf16[1,128,2048]{2,1,0:T(8,128)(2,1)}, u32[]{:S(2)}) copy-start(bf16[1,128,2048]{2,1,0:T(8,128)(2,1)} %param.12) | copy-start | bytes 1572868
  155.8 53.2 %copy-start.24 = (f32[2048]{0:T(1024)S(1)}, f32[2048]{0:T(1024)}, u32[]{:S(2)}) copy-start(f32[2048]{0:T(1024)} %param.17) | copy-start | bytes 24580
  155.8 141.8 %all-gather.12.cloned.1.call-start = ((), (), s32[]{:S(2)}) async-start(), calls=%async_computation.11 | async-start | bytes 8912896 | tf_op jit(solution)/shard_map/all_gather | solution.py:752
  157.9 364.9 %all-gather.14.cloned.1.call-start = ((), (), s32[]{:S(2)}) async-start(), calls=%async_computation.12 | async-start | bytes 2621440 | tf_op jit(solution)/shard_map/all_gather | solution.py:823
  158.1 53.4 %copy-start.23 = (pred[128,16]{1,0:T(8,128)(4,1)}, pred[128,16]{1,0:T(8,128)(4,1)S(1)}, u32[]{:S(2)}) copy-start(pred[128,16]{1,0:T(8,128)(4,1)S(1)} %copy.56) | copy-start | bytes 6148
  207.1 5.2 copy-start.7
  209.0 4.5 copy-start.33
  466.9 4.9 copy-start.51
  466.9 5.9 copy-start.5
  466.9 5.8 copy-start.8
  466.9 5.8 copy-start.13
  466.9 5.8 copy-start.25
  467.0 5.8 copy-start.34
  468.2 5.8 copy-start.46
  471.8 1.0 copy-start.10
  471.8 2.2 copy-start.44
  472.8 50.0 %copy-start.53 = (bf16[512,2048]{1,0:T(8,128)(2,1)S(1)}, bf16[512,2048]{1,0:T(8,128)(2,1)}, u32[]{:S(2)}) copy-start(bf16[512,2048]{1,0:T(8,128)(2,1)} %param.16) | copy-start | bytes 6291460
  474.0 119.6 %reduce-scatter.10.cloned.1.call-start = ((), (), s32[]{:S(2)}) async-start(), calls=%async_computation.13 | async-start | bytes 2621440 | tf_op jit(solution)/shard_map/reduce_scatter | solution.py:831
  548.4 72.9 %reduce-scatter.12.cloned.1.call-start = ((), (), s32[]{:S(2)}) async-start(), calls=%async_computation.14 | async-start | bytes 2621440 | tf_op jit(solution)/shard_map/reduce_scatter | solution.py:834
  549.2 243.3 %reduce-scatter.20.cloned.1.call-start = ((), (), s32[]{:S(2)}) async-start(), calls=%async_computation.19 | async-start | bytes 6291456 | tf_op jit(solution)/shard_map/reduce_scatter | solution.py:792
  563.3 233.3 %reduce-scatter.18.cloned.1.call-start = ((), (), s32[]{:S(2)}) async-start(), calls=%async_computation.18 | async-start | bytes 6291456 | tf_op jit(solution)/shard_map/reduce_scatter | solution.py:792
  577.6 223.4 %reduce-scatter.16.cloned.1.call-start = ((), (), s32[]{:S(2)}) async-start(), calls=%async_computation.17 | async-start | bytes 6291456 | tf_op jit(solution)/shard_map/reduce_scatter | solution.py:792
  591.8 1.5 copy-start.19
  591.8 3.1 copy-start.16
  591.8 3.1 copy-start.18
  591.8 213.5 %reduce-scatter.14.cloned.1.call-start = ((), (), s32[]{:S(2)}) async-start(), calls=%async_computation.15 | async-start | bytes 2621440 | tf_op jit(solution)/shard_map/reduce_scatter | solution.py:842
  594.9 1.6 copy-start.3
  594.9 1.6 copy-start.22
  594.9 1.6 copy-start.31
  596.5 0.7 copy-start.29
  629.0 1.1 copy-start.20
  629.1 5.5 copy-start.56
  629.1 186.6 %all-reduce.9.cloned.1.call-start = ((), (), s32[]{:S(2)}) async-start(), calls=%async_computation.20 | async-start | bytes 16777216 | tf_op jit(solution)/shard_map/psum | solution.py:854
  630.1 4.4 copy-start.55
  640.0 0.7 copy-start.35
  640.0 0.7 copy-start.37
  640.0 0.7 copy-start.39
  640.0 307.6 %all-reduce.7.cloned.1.call-start = ((), (), s32[]{:S(2)}) async-start(), calls=%async_computation.16 | async-start | bytes 262144 | tf_op jit(solution)/shard_map/psum | solution.py:858
  800.9 4.4 copy-start.6
  800.9 4.4 copy-start.27
  800.9 4.4 copy-start.41
  800.9 6.0 copy-start.49
  800.9 6.1 copy-start.9
  800.9 6.1 copy-start.11
  800.9 6.1 copy-start.14
  801.0 6.1 copy-start.45
  819.8 9.5 copy-start.32
  819.8 129.3 %copy-start.1 = (f32[2048,16]{0,1:T(8,128)S(1)}, f32[2048,16]{0,1:T(8,128)}, u32[]{:S(2)}) copy-start(f32[2048,16]{0,1:T(8,128)} %param.18) | copy-start | bytes 393220
  (7 other events, 4.1 us)
Sparse Core Ops, SparseCore 0:
  12.6 48.3 all-gather.5
  65.6 33.9 all-gather.9
  102.0 35.1 all-gather.7
  155.9 51.1 reduce-scatter.7
  474.1 48.6 all-gather.13
  548.6 33.9 reduce-scatter.9
  586.1 35.1 reduce-scatter.11
  624.2 12.0 reduce-scatter.19
  639.1 13.3 reduce-scatter.17
  655.2 13.2 reduce-scatter.15
  671.4 62.6 reduce-scatter.13
Sparse Core Ops, SparseCore 1:
  159.7 137.9 all-gather.11
  640.1 175.6 all-reduce.8
  821.7 125.8 all-reduce.6

commit v3 on v2

--- a/solution.py
+++ b/solution.py
@@ -254,6 +254,9 @@
     def front_id(self):
         return {"context": self.front}
 
+    def pair_id(self):
+        return {"dp": 1 - lax.axis_index("dp")}
+
     def above_id(self):
         return {"expert": jnp.minimum(self.lev + 1, GROUP - 1)}
 
@@ -266,7 +269,7 @@
         level = jnp.where(near == 0, rank, jnp.where(rank < 2, 1 - rank, rank))
         return jnp.where(flipped, GROUP - 1 - level, level)
 
-    def greet(self, plane=True, line=True):
+    def greet(self, plane=True, line=True, pair=False):
         barrier = pltpu.get_barrier_semaphore()
 
         def call(target):
@@ -278,7 +281,9 @@
         if line:
             pl.when(self.has_above)(lambda: call(self.above_id()))
             pl.when(self.has_below)(lambda: call(self.below_id()))
-        peers = 2 if plane else 0
+        if pair:
+            call(self.pair_id())
+        peers = (2 if plane else 0) + (1 if pair else 0)
         if line:
             peers = peers + 1 + jnp.where((self.lev > 0) & (self.lev < GROUP - 1), 1, 0)
         pl.semaphore_wait(barrier, peers)
@@ -540,17 +545,20 @@
     )(sending, all_upstream, w_gate, w_up, w_down)
 
 
-def give_back_kernel(tok, width, terms, tailed, *refs):
+def give_back_kernel(tok, width, terms, tailed, graded, *refs):
     refs = list(refs)
     take = lambda n: [refs.pop(0) for _ in range(n)]
     lhs_in, w_in = take(terms), take(terms)
     tail_ref = take(1)[0] if tailed else None
+    grad_in = take(4) if graded else []
     out_ref = take(1)[0]
+    grad_out = take(3) if graded else []
     lhs, weight = take(terms), take(terms)
     (
         mine, part_a, part_b, from_side, from_front, from_above, from_below,
         load_sem, part_send, part_recv, plane_send, plane_recv, line_send, line_recv,
-    ) = refs
+    ) = take(14)
+    grads = WeightGrads(grad_in, grad_out, lhs[0], refs) if graded else None
     at = Place()
     half = tok // 2
     wide = mine.shape[1]
@@ -562,7 +570,9 @@
     ]
     for load in loads:
         load.start()
-    at.greet()
+    if graded:
+        grads.begin()
+    at.greet(pair=graded)
     for load in loads:
         load.wait()
 
@@ -642,6 +652,8 @@
             compute(level, 1)
             part_copy(level, 2).start()
             part_copy(level, 1).start()
+            if graded:
+                grads.tiles(rank * 3, 2)
 
         @pl.when(rank >= 1)
         def _():
@@ -657,10 +669,14 @@
             part_copy(level, 1).wait_recv()
             add_into(slot(level, 2, tok, half, half), part_b[level])
             plane_copy(level, 2).start()
+            if graded:
+                grads.tiles(rank * 3 + 2, 1)
 
         return carry
 
     lax.fori_loop(0, GROUP + 1, step, 0)
+    if graded:
+        grads.end()
 
     def drain(level, carry):
         for member in (1, 2):
@@ -673,7 +689,142 @@
     lax.fori_loop(0, GROUP, drain, 0)
 
 
-def give_back(lhs, weights, tail, ident, name):
+class WeightGrads:
+    def __init__(self, given, outs, hidden, refs):
+        self.feats_in, self.ups_in, self.dgate_in, self.dup_in = given
+        self.outs = outs
+        self.hidden = hidden
+        (
+            self.left, self.dgate, self.dup, self.turned, self.sent, self.got, self.stage,
+            self.load_sem, self.send_sem, self.recv_sem, self.out_sem,
+        ) = refs
+        self.pair = lax.axis_index("dp")
+        self.size = self.turned.shape[0]
+        self.wide = self.dgate.shape[1]
+
+    def loads(self):
+        return [
+            pltpu.make_async_copy(self.feats_in, self.left, self.load_sem.at[0]),
+            pltpu.make_async_copy(self.dgate_in, self.dgate, self.load_sem.at[1]),
+            pltpu.make_async_copy(self.dup_in, self.dup, self.load_sem.at[2]),
+        ]
+
+    def begin(self):
+        for load in self.loads():
+            load.start()
+
+    def last_load(self):
+        return pltpu.make_async_copy(self.ups_in, self.left, self.load_sem.at[3])
+
+    def send(self, piece, place):
+        return remote(
+            self.sent.at[place], self.got.at[piece],
+            self.send_sem.at[piece], self.recv_sem.at[piece],
+            {"dp": 1 - self.pair},
+        )
+
+    def puts(self, piece, place):
+        rows = pl.ds(pl.multiple_of(piece * self.size, self.size), self.size)
+        halves = [
+            pltpu.make_async_copy(
+                self.stage.at[place, :, pl.ds(i * self.wide, self.wide)],
+                self.outs[i].at[rows], self.out_sem.at[i, piece],
+            )
+            for i in range(2)
+        ]
+        return halves
+
+    def last_put(self, piece, place):
+        rows = pl.ds(pl.multiple_of((piece - 4) * self.size, self.size), self.size)
+        return pltpu.make_async_copy(
+            self.stage.at[place], self.outs[2].at[rows], self.out_sem.at[2, piece]
+        )
+
+    def each_put(self, piece, place, act):
+        @pl.when(piece < 4)
+        def _():
+            for copy in self.puts(piece, place):
+                act(copy)
+
+        pl.when(piece >= 4)(lambda: act(self.last_put(piece, place)))
+
+    def tile(self, index):
+        late = index >= 8
+        inner = index - jnp.where(late, 8, 0)
+        count = jnp.where(late, 2, 4)
+        own = inner >= count
+        local = jnp.where(own, inner - count, inner)
+        piece = local + jnp.where(late, 4, 0)
+        owner = jnp.where(own, self.pair, 1 - self.pair)
+        cols = pl.ds(pl.multiple_of((owner * count + local) * self.size, self.size), self.size)
+        place = local % 2
+        keep = lambda copy: copy.wait()
+
+        @pl.when(index == 0)
+        def _():
+            for load in self.loads():
+                load.wait()
+
+        @pl.when(index == 8)
+        def _():
+            self.last_load().start()
+            self.last_load().wait()
+
+        pl.when(late)(lambda: self.turn(self.hidden, cols))
+        pl.when(jnp.logical_not(late))(lambda: self.turn(self.left, cols))
+
+        pl.when(jnp.logical_not(own) & (piece >= 2))(lambda: self.send(piece - 2, place).wait_send())
+
+        @pl.when(own)
+        def _():
+            pl.when(piece >= 2)(lambda: self.each_put(piece - 2, place, keep))
+            self.send(piece, place).wait_recv()
+
+        def column(step, carry):
+            width = 512
+            outs = pl.ds(pl.multiple_of(step * width, width), width)
+            per = self.wide // width
+
+            def emit(right):
+                value = nn_dot(self.turned[...], right)
+
+                @pl.when(own)
+                def _():
+                    self.stage[place, :, outs] = value + self.got[piece, :, outs].astype(
+                        jnp.float32
+                    )
+
+                @pl.when(jnp.logical_not(own))
+                def _():
+                    self.sent[place, :, outs] = value.astype(jnp.bfloat16)
+
+            narrow = pl.ds(pl.multiple_of((step % per) * width, width), width)
+            pl.when(late)(lambda: emit(self.left[:, outs]))
+            pl.when(jnp.logical_not(late) & (step < per))(lambda: emit(self.dgate[:, narrow]))
+            pl.when(jnp.logical_not(late) & (step >= per))(lambda: emit(self.dup[:, narrow]))
+            return carry
+
+        lax.fori_loop(0, 2 * self.wide // 512, column, 0)
+        pl.when(own)(lambda: self.each_put(piece, place, lambda copy: copy.start()))
+        pl.when(jnp.logical_not(own))(lambda: self.send(piece, place).start())
+
+    def turn(self, source, cols):
+        self.turned[...] = jnp.transpose(source[:, cols])
+
+    def tiles(self, first, count):
+        def one(step, carry):
+            self.tile(first + step)
+            return carry
+
+        lax.fori_loop(0, count, one, 0)
+
+    def end(self):
+        for piece in (4, 5):
+            self.send(piece, piece % 2).wait_send()
+            self.last_put(piece, piece % 2).wait()
+
+
+def give_back(lhs, weights, tail, ident, name, graded=()):
     total, ff = lhs[0].shape
     terms = len(lhs)
     width = weights[0].shape[0] if terms == 2 else weights[0].shape[1]
@@ -684,11 +835,35 @@
     anywhere = pl.BlockSpec(memory_space=pl.ANY)
     vmem = pl.BlockSpec(memory_space=pltpu.VMEM)
     tails = () if tail is None else (tail,)
+    grad_shapes, grad_scratch = [], []
+    if graded:
+        f32 = jnp.float32
+        size = ff // 4
+        grad_shapes = [
+            jax.ShapeDtypeStruct((width // 2, ff), f32),
+            jax.ShapeDtypeStruct((width // 2, ff), f32),
+            jax.ShapeDtypeStruct((ff // 2, width), f32),
+        ]
+        grad_scratch = [
+            pltpu.VMEM((total, width), bf16),
+            pltpu.VMEM((total, ff), bf16),
+            pltpu.VMEM((total, ff), bf16),
+            pltpu.VMEM((size, total), bf16),
+            pltpu.VMEM((2, size, width), bf16),
+            pltpu.VMEM((6, size, width), bf16),
+            pltpu.VMEM((2, size, width), f32),
+            dma((4,)),
+            dma((6,)),
+            dma((6,)),
+            dma((3, 6)),
+        ]
     return pl.pallas_call(
-        functools.partial(give_back_kernel, tok, width, terms, tail is not None),
-        in_specs=[anywhere] * (2 * terms) + [vmem] * len(tails),
-        out_specs=vmem,
-        out_shape=jax.ShapeDtypeStruct((tok, wide), jnp.float32),
+        functools.partial(
+            give_back_kernel, tok, width, terms, tail is not None, bool(graded)
+        ),
+        in_specs=[anywhere] * (2 * terms) + [vmem] * len(tails) + [anywhere] * len(graded),
+        out_specs=[vmem] + [anywhere] * len(grad_shapes),
+        out_shape=[jax.ShapeDtypeStruct((tok, wide), jnp.float32)] + grad_shapes,
         scratch_shapes=[pltpu.VMEM((total, ff), bf16)] * terms
         + [pltpu.VMEM(w.shape, bf16) for w in weights]
         + [
@@ -706,7 +881,8 @@
             dma((2, GROUP)),
             dma((2, GROUP)),
             dma((2, GROUP)),
-        ],
+        ]
+        + grad_scratch,
         compiler_params=pltpu.CompilerParams(
             collective_id=ident, has_side_effects=True, vmem_limit_bytes=VMEM_BYTES
         ),
@@ -714,10 +890,275 @@
             flops=2 * terms * total * width * ff, bytes_accessed=20 << 20, transcendentals=0
         ),
         name=name,
-    )(*lhs, *weights, *tails)
+    )(*lhs, *weights, *tails, *graded)
+
+
+def line_gather_kernel(tok, x_ref, out_ref, send_sem, recv_sem):
+    at = Place()
+    place = lambda level: pl.ds(pl.multiple_of(level * tok, tok), tok)
+
+    def each(rank, level, act):
+        source = x_ref if isinstance(rank, int) and rank == 0 else out_ref.at[place(level)]
+
+        def copy(up):
+            return remote(
+                source, out_ref.at[place(level)],
+                send_sem.at[0 if up else 1, rank], recv_sem.at[level],
+                at.above_id() if up else at.below_id(),
+            )
+
+        pl.when((level <= at.lev) & at.has_above)(lambda: act(copy(True)))
+        pl.when((level >= at.lev) & at.has_below)(lambda: act(copy(False)))
+
+    at.greet(plane=False)
+    each(0, at.lev, lambda copy: copy.start())
+    out_ref[place(at.lev), :] = x_ref[...]
+
+    def step(rank, carry):
+        level = at.nearest(rank)
+        target = out_ref.at[place(level)]
+        remote(target, target, send_sem.at[0, rank], recv_sem.at[level], at.above_id()).wait_recv()
+        each(rank, level, lambda copy: copy.start())
+        return carry
+
+    lax.fori_loop(1, GROUP, step, 0)
+    each(0, at.lev, lambda copy: copy.wait_send())
+
+    def drain(rank, carry):
+        each(rank, at.nearest(rank), lambda copy: copy.wait_send())
+        return carry
+
+    lax.fori_loop(1, GROUP, drain, 0)
+
+
+def remote_call(kernel, outs, scratch, ident, name, *args):
+    vmem = pl.BlockSpec(memory_space=pltpu.VMEM)
+    return pl.pallas_call(
+        kernel,
+        in_specs=[vmem] * len(args),
+        out_specs=[vmem] * len(outs),
+        out_shape=outs,
+        scratch_shapes=scratch,
+        compiler_params=pltpu.CompilerParams(
+            collective_id=ident, has_side_effects=True, vmem_limit_bytes=32 << 20
+        ),
+        cost_estimate=pl.CostEstimate(flops=0, bytes_accessed=100 << 20, transcendentals=0),
+        name=name,
+    )(*args)
+
+
+def line_gather(values, ident, name):
+    tok, width = values.shape
+    dma = pltpu.SemaphoreType.DMA
+    return remote_call(
+        functools.partial(line_gather_kernel, tok),
+        [jax.ShapeDtypeStruct((GROUP * tok, width), values.dtype)],
+        [dma((2, GROUP)), dma((GROUP,))],
+        ident, name, values,
+    )[0]
+
+
+def line_scatter_kernel(tok, x_ref, out_ref, carry_up, carry_down, above, below, send_sem, recv_sem):
+    at = Place()
+    place = lambda level: pl.ds(pl.multiple_of(level * tok, tok), tok)
+
+    def copy(level, up):
+        return remote(
+            (carry_up if up else carry_down).at[level], (below if up else above).at[level],
+            send_sem.at[0 if up else 1, level], recv_sem.at[0 if up else 1, level],
+            at.above_id() if up else at.below_id(),
+        )
+
+    at.greet(plane=False)
+
+    def step(rank, carry):
+        level = at.nearest(GROUP - 1 - rank)
+        out_ref[...] = x_ref[place(level), :].astype(jnp.float32)
+
+        @pl.when((level <= at.lev) & at.has_above)
+        def _():
+            copy(level, False).wait_recv()
+            out_ref[...] += above[level].astype(jnp.float32)
+
+        @pl.when((level >= at.lev) & at.has_below)
+        def _():
+            copy(level, True).wait_recv()
+            out_ref[...] += below[level].astype(jnp.float32)
+
+        @pl.when(level < at.lev)
+        def _():
+            carry_down[level] = out_ref[...].astype(jnp.bfloat16)
+            copy(level, False).start()
+
+        @pl.when(level > at.lev)
+        def _():
+            carry_up[level] = out_ref[...].astype(jnp.bfloat16)
+            copy(level, True).start()
+
+        return carry
+
+    lax.fori_loop(0, GROUP, step, 0)
+
+    def drain(level, carry):
+        pl.when(level < at.lev)(lambda: copy(level, False).wait_send())
+        pl.when(level > at.lev)(lambda: copy(level, True).wait_send())
+        return carry
+
+    lax.fori_loop(0, GROUP, drain, 0)
+
+
+def line_scatter(values, ident, name):
+    rows, width = values.shape
+    tok = rows // GROUP
+    dma = pltpu.SemaphoreType.DMA
+    return remote_call(
+        functools.partial(line_scatter_kernel, tok),
+        [jax.ShapeDtypeStruct((tok, width), jnp.float32)],
+        [pltpu.VMEM((GROUP, tok, width), jnp.bfloat16)] * 4
+        + [dma((2, GROUP)), dma((2, GROUP))],
+        ident, name, values,
+    )[0]
+
+
+def plane_gather_kernel(rows, count, *refs):
+    xs, outs = refs[:count], refs[count : 2 * count]
+    send_sem, recv_sem = refs[2 * count :]
+    at = Place()
+    half = rows // 2
+    place = lambda column, start, size: pl.ds(pl.multiple_of(column * rows + start, half), size)
+
+    def full(i, member):
+        return remote(
+            xs[i], outs[i].at[place(at.ctx, 0, rows)],
+            send_sem.at[i, member], recv_sem.at[i, member],
+            at.side_id() if member == 0 else at.front_id(),
+        )
+
+    def part(i, member):
+        column = at.side if member == 0 else at.front
+        source = outs[i].at[place(column, member * half, half)]
+        return remote(
+            source, source, send_sem.at[i, 2 + member], recv_sem.at[i, 2 + member],
+            at.front_id() if member == 0 else at.side_id(),
+        )
+
+    at.greet(line=False)
+    for i in range(count):
+        full(i, 0).start()
+        full(i, 1).start()
+    for i in range(count):
+        outs[i][place(at.ctx, 0, rows), :] = xs[i][...]
+    for i in range(count):
+        for member in range(2):
+            full(i, member).wait_recv()
+            part(i, member).start()
+    for i in range(count):
+        for member in range(2):
+            part(i, member).wait_recv()
+    for i in range(count):
+        for member in range(2):
+            full(i, member).wait_send()
+            part(i, member).wait_send()
+
+
+def plane_gather(values, ident, name):
+    rows, width = values[0].shape
+    count = len(values)
+    dma = pltpu.SemaphoreType.DMA
+    return remote_call(
+        functools.partial(plane_gather_kernel, rows, count),
+        [jax.ShapeDtypeStruct((GROUP * rows, width), v.dtype) for v in values],
+        [dma((count, 4)), dma((count, 4))],
+        ident, name, *values,
+    )
+
+
+def plane_scatter_kernel(rows, count, *refs):
+    xs, outs = refs[:count], refs[count : 2 * count]
+    added, parts, fulls = refs[2 * count : 5 * count : 3], refs[2 * count + 1 : 5 * count : 3], refs[2 * count + 2 : 5 * count : 3]
+    send_sem, recv_sem = refs[5 * count :]
+    at = Place()
+    half = rows // 2
+    place = lambda column, start, size: pl.ds(pl.multiple_of(column * rows + start, half), size)
+    columns = (at.side, at.front)
+    nears = (at.side_id(), at.front_id())
+
+    def part(i, member):
+        return remote(
+            xs[i].at[place(GROUP - 1 - at.ctx, (1 - member) * half, half)], parts[i].at[member],
+            send_sem.at[i, member], recv_sem.at[i, member], nears[member],
+        )
+
+    def plain(i, member):
+        start = (1 - member) * half
+        return remote(
+            xs[i].at[place(columns[member], start, half)], fulls[i].at[member, pl.ds(start, half)],
+            send_sem.at[i, 2 + member], recv_sem.at[i, 2 + member], nears[member],
+        )
+
+    def summed(i, member):
+        start = member * half
+        return remote(
+            added[i].at[member], fulls[i].at[member, pl.ds(start, half)],
+            send_sem.at[i, 4 + member], recv_sem.at[i, 4 + member], nears[member],
+        )
+
+    at.greet(line=False)
+    for i in range(count):
+        for member in range(2):
+            part(i, member).start()
+        for member in range(2):
+            plain(i, member).start()
+    for i in range(count):
+        for member in range(2):
+            part(i, 1 - member).wait_recv()
+            own = xs[i][place(columns[member], member * half, half), :]
+            added[i][member] = (
+                own.astype(jnp.float32) + parts[i][1 - member].astype(jnp.float32)
+            ).astype(jnp.bfloat16)
+            summed(i, member).start()
+    for i in range(count):
+        total = xs[i][place(at.ctx, 0, rows), :].astype(jnp.float32)
+        for member in range(2):
+            plain(i, member).wait_recv()
+            summed(i, member).wait_recv()
+            total = total + fulls[i][member].astype(jnp.float32)
+        outs[i][...] = total
+    for i in range(count):
+        for member in range(2):
+            part(i, member).wait_send()
+            plain(i, member).wait_send()
+            summed(i, member).wait_send()
+
+
+def plane_scatter(values, ident, name):
+    rows, width = values[0].shape
+    rows = rows // GROUP
+    count = len(values)
+    dma = pltpu.SemaphoreType.DMA
+    bf16 = jnp.bfloat16
+    return remote_call(
+        functools.partial(plane_scatter_kernel, rows, count),
+        [jax.ShapeDtypeStruct((rows, width), jnp.float32) for _ in values],
+        [
+            pltpu.VMEM((2, rows // 2, width), bf16),
+            pltpu.VMEM((2, rows // 2, width), bf16),
+            pltpu.VMEM((2, rows, width), bf16),
+        ]
+        * count
+        + [dma((count, 6)), dma((count, 6))],
+        ident, name, *values,
+    )
 
 
 TOKEN_AXES = ("context", "expert")
+
+
+def small_sums(router_part, moe_gain_part):
+    width, experts = router_part.shape
+    packed = jnp.concatenate([jnp.transpose(router_part), moe_gain_part[None]], axis=0)
+    total = lax.psum(packed, ("dp", "context", "expert"))
+    return jnp.transpose(total[:experts]), total[experts]
 
 
 def fast_device(
@@ -748,7 +1189,7 @@
     )
 
     normed_b = rms_scale(tokens, attn_gain).astype(jnp.bfloat16)
-    gathered_in = lax.all_gather(normed_b, "expert", axis=0, tiled=True)
+    gathered_in = line_gather(normed_b, 4, "gather_normed")
     all_upstream = lax.all_gather(
         upstream.astype(jnp.bfloat16), TOKEN_AXES, axis=0, tiled=True
     )
@@ -762,12 +1203,9 @@
 
     rotated = prep_local(projected, qk_gain).astype(jnp.bfloat16)
     feat_width = projected.shape[2]
-    keys_all = lax.all_gather(rotated[1], "context", axis=0, tiled=True)
-    values_all = lax.all_gather(value_local, "context", axis=0, tiled=True)
+    keys_all, values_all = plane_gather((rotated[1], value_local), 5, "gather_keys")
     attended, lse = attend(place, rotated[0], keys_all, values_all, context_size)
-    branch_out = lax.psum_scatter(
-        nn_dot(attended, w_out).astype(jnp.bfloat16), "expert", scatter_dimension=0, tiled=True
-    ).astype(jnp.float32)
+    branch_out = line_scatter(nn_dot(attended, w_out).astype(jnp.bfloat16), 6, "sum_heads")
     resid = tokens + branch_out
     mixed_in = rms_scale(resid, moe_gain)
     logits = jnp.dot(
@@ -785,18 +1223,7 @@
     rows, upstream_rows, hidden_w, grad_gate, grad_up, d_pairs = run_experts(
         sending, all_upstream, w_gate[0], w_up[0], w_down[0]
     )
-    returned = give_back((grad_gate, grad_up), (w_gate[0], w_up[0]), d_pairs, 2, "give_back")
-    hidden_out = resid + give_back((hidden_w,), (w_down[0],), None, 3, "combine")
-
-    def over_sequences(grad):
-        return lax.psum_scatter(
-            grad.astype(jnp.bfloat16)[None], "dp", scatter_dimension=1, tiled=True
-        ).astype(jnp.float32)
-
-    gate_sum = over_sequences(tn_dot(rows, grad_gate))
-    up_sum = over_sequences(tn_dot(rows, grad_up))
-    down_sum = over_sequences(tn_dot(hidden_w, upstream_rows))
-
+    returned = give_back((grad_gate, grad_up), (w_gate[0], w_up[0]), d_pairs, 2, "give_back")[0]
     d_weights = (
         returned[:, model_width : model_width + expert_count]
         + returned[:, model_width + expert_count : model_width + 2 * expert_count]
@@ -820,44 +1247,48 @@
     _, second_pull = jax.vjp(rms_scale, resid, moe_gain)
     resid_part, moe_gain_part = second_pull(d_mixed)
     d_resid = upstream + resid_part
-    grad_gathered = lax.all_gather(
-        d_resid.astype(jnp.bfloat16), "expert", axis=0, tiled=True
-    )
+    router_sum, moe_sum = small_sums(router_part, moe_gain_part)
+    grad_gathered = line_gather(d_resid.astype(jnp.bfloat16), 7, "gather_resid")
     out_grad = tn_dot(attended, grad_gathered)
     d_attended = nt_dot(grad_gathered, w_out).astype(jnp.bfloat16)
     d_queries, key_part, value_part = attend_back(
         place, rotated[0], d_attended, attended, lse, keys_all, values_all, context_size
     )
-    key_grad = lax.psum_scatter(
-        key_part, "context", scatter_dimension=0, tiled=True
-    ).astype(jnp.float32)
-    value_grad = lax.psum_scatter(
-        value_part, "context", scatter_dimension=0, tiled=True
-    ).astype(jnp.float32)
+    key_grad, value_grad = plane_scatter((key_part, value_part), 8, "sum_keys")
     d_rotated = jnp.stack([d_queries, key_grad])
     _, prep_pull = jax.vjp(prep_local, projected, qk_gain)
     d_pair, qk_part = prep_pull(d_rotated)
     d_proj = jnp.concatenate([d_pair, value_grad[None]], axis=0).astype(jnp.bfloat16)
     qkv_grad = jnp.einsum("rd,krf->kdf", gathered_in, d_proj, preferred_element_type=jnp.float32)
-    d_normed = lax.psum_scatter(
+    d_normed = line_scatter(
         jnp.einsum("krf,kdf->rd", d_proj, w_qkv, preferred_element_type=jnp.float32).astype(
             jnp.bfloat16
         ),
-        "expert",
-        scatter_dimension=0,
-        tiled=True,
-    ).astype(jnp.float32)
+        9,
+        "sum_normed",
+    )
     _, first_pull = jax.vjp(rms_scale, tokens, attn_gain)
     token_part, attn_gain_part = first_pull(d_normed)
     grad_in = d_resid + token_part
-    qkv_sum, out_sum, qk_sum = (
+    combined, gate_sum, up_sum, down_sum = give_back(
+        (hidden_w,), (w_down[0],), None, 3, "combine",
+        graded=(rows, upstream_rows, grad_gate, grad_up),
+    )
+    hidden_out = resid + combined
+    qkv_sum, out_sum = (
         lax.psum(qkv_grad.astype(jnp.bfloat16), ("dp", "context")).astype(jnp.float32),
         lax.psum(out_grad.astype(jnp.bfloat16), ("dp", "context")).astype(jnp.float32),
-        lax.psum(qk_part.astype(jnp.bfloat16), ("dp", "context")).astype(jnp.float32),
-    )
-    attn_sum, moe_sum, router_sum = lax.psum(
-        (attn_gain_part, moe_gain_part, router_part), ("dp", "context", "expert")
-    )
+    )
+    qk_slots = jnp.where(
+        jnp.arange(expert_size)[:, None] == lax.axis_index("expert"), qk_part.reshape(1, -1), 0.0
+    )
+    last = lax.psum(
+        jnp.concatenate([attn_gain_part, qk_slots.reshape(-1)]), ("dp", "context", "expert")
+    )
+    attn_sum = last[:model_width]
+    qk_sum = lax.dynamic_index_in_dim(
+        last[model_width:].reshape(expert_size, -1), lax.axis_index("expert"), 0, keepdims=False
+    ).reshape(qk_part.shape)
     return (
         hidden_out[None],
         grad_in[None],
@@ -867,9 +1298,9 @@
         out_sum,
         moe_sum,
         router_sum,
-        gate_sum,
-        up_sum,
-        down_sum,
+        gate_sum[None],
+        up_sum[None],
+        down_sum[None],
     )
 
 

time: 966 us -> 762 us (0.79)
  waiting for transfers between devices: 390 us -> 38.3 us
  Pallas kernels: 338 us -> 569 us
  matrix products: 83.4 us -> 34 us
  blocking collectives: 68.1 us -> 41.2 us
  local copies, waits for them, and re-layouts: 26 us -> 44.4 us
  other arithmetic: 33.8 us -> 19.7 us
    pallas_call x0 -> x6, Pallas kernels: none -> 274 us  [remote_call(): pl.pallas_call(kernel, in_specs=[vmem] * len(args), out_specs=[vmem] * le...]
    all_gather x4 -> x0, waiting for transfers between devices: 160 us -> none  [the longest x1 48.7 us: fast_device(): lax.all_gather(d_resid.astype(jnp.bfloat16), 'expert', axis=0, tiled=True)]
    all_gather x1, waiting for transfers between devices: 84 us -> 0.01 us  [fast_device(): lax.all_gather(upstream.astype(jnp.bfloat16), TOKEN_AXES, axis=0, tiled=T...]
    reduce_scatter x7 -> x0, waiting for transfers between devices: 72.2 us -> none  [the longest x1 49.1 us: fast_device(): lax.psum_scatter(nn_dot(attended, w_out).astype(jnp.bfloat16), 'expert',...]
    psum x1, waiting for transfers between devices: 67.9 us -> 0.01 us  [small_sums(): total = lax.psum(packed, ('dp', 'context', 'expert'))]
    dot_general x4 -> x1, matrix products: 46.6 us -> 2.6 us  [tn_dot(): lax.dot_general(left, right, (((0,), (0,)), ((), ())), preferred_element_...]
    pallas_call x2, Pallas kernels: 218 us -> 176 us  [give_back(): pl.pallas_call(functools.partial(give_back_kernel, tok, width, terms, tai...]
    psum x1, waiting for transfers between devices: 5.32 us -> 38.2 us  [fast_device(): lax.psum(qkv_grad.astype(jnp.bfloat16), ('dp', 'context'))]
  transfers between devices with their start and end apart: 14 -> 3, of which waited for: 9 -> 1; matrix products, arithmetic and copies ran while one was open for 12% -> 7% of each run, Pallas kernels for 14% -> 53%
where the time goes in v3:
time: 762 us; the launch traced here: 761 us
  Pallas kernels  569 us (75%)
  local copies, waits for them, and re-layouts  44.4 us (6%)
  blocking collectives  41.2 us (5%)
  waiting for transfers between devices  38.3 us (5%)
  matrix products  34 us (4%)
  other arithmetic  19.7 us (3%)
  between operations  14.5 us (2%)
    pallas_call x6, Pallas kernels, remote_call(): pl.pallas_call(kernel, in_specs=[vmem] * len(args), out_specs=[vmem] * le...  274 us
    pallas_call x2, Pallas kernels, give_back(): pl.pallas_call(functools.partial(give_back_kernel, tok, width, terms, tai...  176 us
    pallas_call x1, Pallas kernels, run_experts(): pl.pallas_call(functools.partial(experts_kernel, tok, width, GROUP * GROU...  82.5 us
    psum x1, blocking collectives, fast_device(): lax.psum(jnp.concatenate([attn_gain_part, qk_slots.reshape(-1)]), ('dp',...  41.2 us
    psum x1, waiting for transfers between devices, fast_device(): lax.psum(qkv_grad.astype(jnp.bfloat16), ('dp', 'context'))  38.2 us
    unnamed x121, local copies, waits for them, and re-layouts  28.9 us
    pallas_call x1, Pallas kernels, attend_back(): pl.pallas_call(functools.partial(attend_back_kernel, blocks, half), grid=...  21.9 us
  transfers between devices with their start and end apart: 3, of which 1 were waited for; matrix products, arithmetic and copies ran while one was open for 7% of the time, Pallas kernels for 53%

profile of v3, /device:TPU:0, one launch (start us, length us, event | category | flops | bytes accessed | tf_op | source)
XLA Modules:
  0.0 761.1 jit_solution(9970758359299177566)
XLA Ops:
  7.3 2.2 bitcast_convert_fusion.1
  9.7 0.2 fusion.18
  10.0 0.2 fusion.13.x_ref
  10.2 74.2 %gather_normed.1 = bf16[512,2048]{1,0:T(8,128)(2,1)S(1)} custom-call(bf16[128,2048]{1,0:T(8,128)(2,1)S(1)} %fusion.13.x_ref), custom_call_target="tpu_custom_call" | custom-call | bytes 104857600 | tf_op jit(solution)/shard_map/gather_normed/pallas_call | solution.py:936
  84.4 5.3 multiply_reduce_fusion.2
  89.8 0.5 multiply_cosine_fusion
  90.4 0.2 multiply_multiply_fusion
  90.6 0.5 copy-done.13
  91.1 0.4 add_convert_fusion
  91.5 1.0 pad_maximum_fusion.4
  92.6 1.3 copy.65.refs_0_
  93.8 2.0 copy.64.q_ref
  95.9 2.8 fusion.8.refs_1_
  98.7 56.7 %gather_keys.1 = (bf16[2048,512]{1,0:T(8,128)(2,1)S(1)}, bf16[2048,512]{1,0:T(8,128)(2,1)S(1)}) custom-call(bf16[512,512]{1,0:T(8,128)(2,1)S(1)} %copy.65.refs_0_, bf16[512,512]{1,0:T(8,128)(2,1)S(1)} %fusion.8.refs_1_), custom_call_target="tpu_custom_call" | custom-call | bytes 104857600 | tf_op jit(solution)/shard_map/gather_keys/pallas_call | solution.py:936
  155.4 1.3 copy-done.2
  156.8 1.3 copy-done.3
  158.1 14.9 %attend.1 = (bf16[512,512]{1,0:T(8,128)(2,1)}, f32[4,1,512]{2,1,0:T(1,128)}) custom-call(s32[1]{0:T(128)} %bitcast.1.place_ref, bf16[512,512]{1,0:T(8,128)(2,1)} %copy.64.q_ref, bf16[2048,512]{1,0:T(8,128)(2,1)} %copy-done.2, bf16[2048,512]{1,0:T(8,128)(2,1)} %copy-done.3), custom_call_target="tpu_custom_call" | custom-call | tf_op jit(solution)/shard_map/attend/pallas_call | solution.py:136
  173.0 2.3 convolution_convert_fusion.1.x_ref
  175.3 38.2 %sum_heads.1 = f32[128,2048]{1,0:T(8,128)S(1)} custom-call(bf16[512,2048]{1,0:T(8,128)(2,1)S(1)} %convolution_convert_fusion.1.x_ref), custom_call_target="tpu_custom_call" | custom-call | bytes 104857600 | tf_op jit(solution)/shard_map/sum_heads/pallas_call | solution.py:936
  213.5 0.2 multiply_reduce_fusion.5
  213.8 0.5 copy-done.54
  214.2 1.0 fusion.47
  215.4 0.2 fusion.31
  215.9 1.0 concatenate.19.x_ref
  216.9 82.5 %experts.1 = (bf16[2048,2048]{1,0:T(8,128)(2,1)}, bf16[2048,2048]{1,0:T(8,128)(2,1)}, bf16[2048,1024]{1,0:T(8,128)(2,1)}, bf16[2048,1024]{1,0:T(8,128)(2,1)}, bf...) custom-call(bf16[128,2176]{1,0:T(8,128)(2,1)} %concatenate.19.x_ref, ...), custom_call_target="tpu_custom_call" | custom-call | flops 25769803776 | bytes 62914560 | tf_op jit(solution)/shard_map/experts/pallas_call | solution.py:505
  299.4 83.7 %give_back.1 = f32[128,2176]{1,0:T(8,128)} custom-call(bf16[2048,1024]{1,0:T(8,128)(2,1)} %get-tuple-element.36.refs_4_.refs_0_, bf16[2048,1024]{1,0:T(8,128)(2,1)} %get-tuple-element.37.refs_5_.refs_1_, bf16[2048,1024]{1,0:T(8,128)(2,1)} %bitcast.92, bf16[2048,1024]{1,0:T(8,128)(2,1)} %bitcast.94, bf16[2048,128]{1,0:T(8,128)(2,1)} %get-tuple-element.39.refs_4_), custom_call_target="tpu_custom_call" | custom-call | flops 17179869184 | bytes 20971520 | tf_op jit(solution)/shard_map/give_back/pallas_call | solution.py:860
  383.1 1.2 multiply_reduce_fusion.6
  384.3 3.8 multiply_reduce_fusion.3
  388.1 0.8 fusion.21
  388.9 0.7 pad_maximum_fusion.5
  389.7 92.1 %combine.1 = (f32[128,2048]{1,0:T(8,128)}, f32[1024,1024]{1,0:T(8,128)}, f32[1024,1024]{1,0:T(8,128)}, f32[512,2048]{1,0:T(8,128)}) custom-call(bf16[2048,1024]{1,0:T(8,128)(2,1)} %get-tuple-element.33.refs_0_, bf16[1024,2048]{1,0:T(8,128)(2,1)} %bitcast.83, bf16[2048,2048]{1,0:T(8,128)(2,1)} %get-tuple-element.34.refs_2_, ...), custom_call_target="tpu_custom_call" | custom-call | flops 8589934592 | bytes 20971520 | tf_op jit(solution)/shard_map/combine/pallas_call | solution.py:860
  481.9 3.9 fusion.45
  485.8 39.0 %gather_resid.1 = bf16[512,2048]{1,0:T(8,128)(2,1)S(1)} custom-call(bf16[128,2048]{1,0:T(8,128)(2,1)S(1)} %get-tuple-element.101.x_ref), custom_call_target="tpu_custom_call" | custom-call | bytes 104857600 | tf_op jit(solution)/shard_map/gather_resid/pallas_call | solution.py:936
  524.8 2.1 convolution_convert_fusion.2.g_ref
  526.9 21.9 %attend_back.1 = (f32[512,512]{1,0:T(8,128)}, bf16[2048,512]{1,0:T(8,128)(2,1)}, bf16[2048,512]{1,0:T(8,128)(2,1)}) custom-call(s32[1]{0:T(128)} %bitcast.1.place_ref, bf16[512,512]{1,0:T(8,128)(2,1)} %copy.64.q_ref, bf16[512,512]{1,0:T(8,128)(2,1)} %convolution_convert_fusion.2.g_ref, bf16[512,512]{1,0:T(8,128)(2,1)} %get-tuple-element.32.o_ref, ...), custom_call_target="tpu_custom_call" | custom-call | tf_op jit(solution)/shard_map/attend_back/pallas_call | solution.py:208
  548.8 2.7 copy.66
  551.5 1.6 copy-done.9
  553.1 31.9 %sum_keys.1 = (f32[512,512]{1,0:T(8,128)S(1)}, f32[512,512]{1,0:T(8,128)S(1)}) custom-call(bf16[2048,512]{1,0:T(8,128)(2,1)S(1)} %copy-done.8, bf16[2048,512]{1,0:T(8,128)(2,1)S(1)} %copy-done.9), custom_call_target="tpu_custom_call" | custom-call | bytes 104857600 | tf_op jit(solution)/shard_map/sum_keys/pallas_call | solution.py:936
  585.0 1.0 copy-done.10
  586.0 1.7 copy.67
  587.7 0.5 multiply_add_fusion.1
  588.2 1.1 copy-done.14
  589.3 0.6 multiply_reduce_fusion
  590.0 1.4 fusion.2
  591.5 2.4 copy.68
  594.0 6.8 convert_bitcast_fusion
  600.8 2.6 convolution_convert_fusion
  603.6 1.1 copy-done.25
  604.8 6.4 bitcast_convert_fusion.x_ref
  611.3 33.7 %sum_normed.1 = f32[128,2048]{1,0:T(8,128)S(1)} custom-call(bf16[512,2048]{1,0:T(8,128)(2,1)S(1)} %bitcast_convert_fusion.x_ref), custom_call_target="tpu_custom_call" | custom-call | bytes 104857600 | tf_op jit(solution)/shard_map/sum_normed/pallas_call | solution.py:936
  645.0 0.4 fusion.14
  645.4 41.2 %psum.28 = f32[6144]{0:T(1024)S(1)} all-reduce(f32[6144]{0:T(1024)S(1)} %pad_maximum_fusion.6), channel_id=1, replica_groups=mesh['dp'=2,'context'=4,'expert'=4] {'dp','context','expert'}, use_global_device_ids=true, to_apply=%region_12.13 | all-reduce | flops 6144 | bytes 49152 | tf_op jit(solution)/shard_map/psum | solution.py:1285
  686.6 0.6 slice.70
  687.3 0.6 reshape.240
  687.9 1.3 fusion.17
  689.2 1.4 slice.72
  690.6 1.6 slice_bitcast_fusion
  692.2 38.2 %all-reduce.8.cloned.1.call-done = (bf16[3,2048,512]{1,2,0:T(8,128)(2,1)}, bf16[512,2048]{1,0:T(8,128)(2,1)}) async-done(((bf16[3,2048,512]{1,2,0:T(8,128)(2,1)}, bf16[512,2048]{1,0:T(8,128)(2,1)}), (bf16[3,2048,512]{1,2,0:T(8,128)(2,1)}, bf16[512,2048]{1,0:T(8,128)(2,1)})) %all-reduce.8.cloned.1.call-update) | async-done | bytes 8388624 | tf_op jit(solution)/shard_map/psum | solution.py:1279
  730.4 4.1 convert_element_type.83
  734.5 9.4 %copy.62 = f32[3,2048,512]{2,1,0:T(8,128)} copy(bf16[3,2048,512]{1,2,0:T(8,128)(2,1)} %get-tuple-element.99) | data formatting | bytes 18874368
  744.0 4.9 copy.79
  748.9 2.1 copy.80
  751.0 1.6 copy-done.18
  752.6 2.0 copy.81
  (138 shorter events, 1.5 us)
Async XLA Ops:
  7.2 207.1 %copy-start = (f32[2048,16]{0,1:T(8,128)S(1)}, f32[2048,16]{0,1:T(8,128)}, u32[]{:S(2)}) copy-start(f32[2048,16]{0,1:T(8,128)} %param.18) | copy-start | bytes 393220
  7.2 2.3 copy-start.51
  7.2 2.4 copy-start.50
  7.2 2.5 copy-start.15
  7.2 2.7 copy-start.35
  7.2 209.6 %all-gather.2.cloned.1.call-start = ((), (), s32[]{:S(2)}) async-start(), calls=%async_computation | async-start | bytes 8912896 | tf_op jit(solution)/shard_map/all_gather | solution.py:1193
  9.5 679.7 %all-reduce.6.cloned.1.call-start = ((), (), s32[]{:S(2)}) async-start(), calls=%async_computation.1 | async-start | bytes 393216 | tf_op jit(solution)/shard_map/psum | solution.py:1160
  9.6 80.8 %copy-start.39 = (f32[2,4,128]{2,1,0:T(4,128)}, f32[2,4,128]{2,1,0:T(4,128)S(1)}, u32[]{:S(2)}) copy-start(f32[2,4,128]{2,1,0:T(4,128)S(1)} %mul.285) | copy-start | bytes 12292
  9.7 205.8 %copy-start.34 = (pred[128,16]{1,0:T(8,128)(4,1)}, pred[128,16]{1,0:T(8,128)(4,1)S(1)}, u32[]{:S(2)}) copy-start(pred[128,16]{1,0:T(8,128)(4,1)S(1)} %copy.56) | copy-start | bytes 6148
  9.9 79.8 %copy-start.52 = (f32[128]{0:T(128)}, f32[128]{0:T(128)S(1)}, u32[]{:S(2)}) copy-start(f32[128]{0:T(128)S(1)} %fusion.18) | copy-start | bytes 1540
  10.0 74.4 %copy-start.48 = (f32[128]{0:T(128)}, f32[128]{0:T(128)S(1)}, u32[]{:S(2)}) copy-start(f32[128]{0:T(128)S(1)} %fusion.39) | copy-start | bytes 1540
  84.4 11.5 %copy-start.4 = (bf16[512,2048]{1,0:T(8,128)(2,1)}, bf16[512,2048]{1,0:T(8,128)(2,1)S(1)}, u32[]{:S(2)}) copy-start(bf16[512,2048]{1,0:T(8,128)(2,1)S(1)} %gather_normed.1) | copy-start | bytes 6291460
  89.7 1.3 copy-start.13
  89.8 1.3 copy-start.37
  89.8 1.3 copy-start.29
  90.3 0.8 copy-start.21
  90.3 0.8 copy-start.23
  155.4 1.3 copy-start.2
  156.8 1.3 copy-start.3
  158.1 14.9 %copy-start.56 = (bf16[512,2048]{1,0:T(8,128)(2,1)S(1)}, bf16[512,2048]{1,0:T(8,128)(2,1)}, u32[]{:S(2)}) copy-start(bf16[512,2048]{1,0:T(8,128)(2,1)} %param.16) | copy-start | bytes 6291460
  213.5 0.7 copy-start.31
  213.7 0.5 copy-start.54
  213.7 3.1 copy-start.11
  214.2 2.6 copy-start.43
  215.3 1.6 copy-start.41
  215.6 1.3 copy-start.46
  383.1 5.0 copy-start.12
  383.1 5.0 copy-start.32
  383.1 5.0 copy-start.42
  383.1 5.0 copy-start.44
  383.1 5.0 copy-start.47
  384.3 4.6 copy-start.55
  389.6 340.7 %all-reduce.8.cloned.1.call-start = ((), (), s32[]{:S(2)}) async-start(), calls=%async_computation.2 | async-start | bytes 16777216 | tf_op jit(solution)/shard_map/psum | solution.py:1279
  389.7 92.2 %copy-start.33 = (f32[2048]{0:T(1024)S(1)}, f32[2048]{0:T(1024)}, u32[]{:S(2)}) copy-start(f32[2048]{0:T(1024)} %param.17) | copy-start | bytes 24580
  389.7 92.2 %copy-start.45 = (f32[128]{0:T(128)S(1)}, f32[128]{0:T(128)}, u32[]{:S(2)}) copy-start(f32[128]{0:T(128)} %copy-done.43) | copy-start | bytes 1540
  485.8 39.0 %copy-start.57 = (bf16[512,2048]{1,0:T(8,128)(2,1)S(1)}, bf16[512,2048]{1,0:T(8,128)(2,1)}, u32[]{:S(2)}) copy-start(bf16[512,2048]{1,0:T(8,128)(2,1)} %param.16) | copy-start | bytes 6291460
  524.8 2.1 copy-start.6
  548.8 2.7 copy-start.8
  551.5 1.6 copy-start.9
  585.0 1.0 copy-start.10
  586.0 1.7 copy-start.17
  586.0 1.7 copy-start.22
  586.0 1.7 copy-start.24
  587.7 1.6 copy-start.14
  587.7 1.6 copy-start.30
  587.7 1.6 copy-start.40
  589.3 0.7 copy-start.38
  591.5 2.5 copy-start.5
  594.0 6.8 copy-start.27
  594.0 6.8 copy-start.7
  594.0 6.8 copy-start.26
  603.4 1.2 copy-start.25
  603.4 1.4 copy-start.28
  611.3 33.8 %copy-start.16 = (bf16[1,128,2048]{2,1,0:T(8,128)(2,1)S(1)}, bf16[1,128,2048]{2,1,0:T(8,128)(2,1)}, u32[]{:S(2)}) copy-start(bf16[1,128,2048]{2,1,0:T(8,128)(2,1)} %param.12) | copy-start | bytes 1572868
  611.3 33.8 %copy-start.36 = (f32[2048]{0:T(1024)S(1)}, f32[2048]{0:T(1024)}, u32[]{:S(2)}) copy-start(f32[2048]{0:T(1024)} %param.13) | copy-start | bytes 24580
  611.3 33.8 %copy-start.49 = (f32[128]{0:T(128)S(1)}, f32[128]{0:T(128)}, u32[]{:S(2)}) copy-start(f32[128]{0:T(128)} %copy-done.48) | copy-start | bytes 1540
  611.3 76.6 %copy-start.53 = (f32[128]{0:T(128)S(1)}, f32[128]{0:T(128)}, u32[]{:S(2)}) copy-start(f32[128]{0:T(128)} %copy-done.52) | copy-start | bytes 1540
  611.3 76.6 %copy-start.20 = (f32[128,2048]{1,0:T(8,128)S(1)}, f32[128,2048]{1,0:T(8,128)}, u32[]{:S(2)}) copy-start(f32[128,2048]{1,0:T(8,128)} %get-tuple-element.102) | copy-start | bytes 3145732
  743.9 4.9 copy-start.19
  748.9 3.7 copy-start.18
  752.6 2.0 copy-start.1
Sparse Core Ops, SparseCore 0:
  11.4 151.3 all-gather.1
  389.8 132.7 all-reduce.5
  603.6 126.7 all-reduce.7
